TPU v7x, 32 devices: a whole 2x2x4 slice. The times are simulated.
32 devices in a mesh: curve: 8 (over z, y), sub: 4 (over x, core).
Axes of the slice: x: 2, y: 2, z: 4, core: 2. Of those that a mesh axis runs over, the one named last changes fastest.
Arguments:
- state: float32 [4, 25, 8192], P(None, None, ('curve', 'sub')), may hold values from -6 to 6
- register: float32 [4, 25, 8192], P(None, None, ('curve', 'sub')), may hold values from -6 to 6
- neighbor: int32 [4, 2048], P(None, ('curve', 'sub')), may hold values from 0 to 2047, as said below
- neighbor_face: int32 [4, 2048], P(None, ('curve', 'sub')), may hold values from 0 to 3, as said below
- seam: int32 [4, 2048], P(None, ('curve', 'sub')), may hold values from 0 to 7, as said below
Outputs:
- next_state: float32 [4, 25, 8192], P(None, None, ('curve', 'sub'))
- next_register: float32 [4, 25, 8192], P(None, None, ('curve', 'sub'))
Inputs may be any that keep to these rules, and one draw needn't show every extreme that they name: neighbor[k, e] is the element across local face k of element e, and the relation is mutual through neighbor_face. Elements d * 64 to (d + 1) * 64 - 1 lie on device d, whose curve index is d // 4 and sub index d % 4. A neighbour lies on the same device; or on one of the two devices with the same curve index and sub index one higher or one lower (wrapping), exactly 8 faces toward each; or on a device with the same sub index whose curve index is 1 to 3 higher or lower (wrapping), 8 such faces in each direction, at most 3 toward any one device. Every device has such faces at distance 3 in both directions, and every device reaches 3 toward some device. neighbor_face[k, e] is the face of neighbor[k, e] whose neighbour is e. seam = rot + 4 * flip; the two faces of a pair carry rot and (4 - rot) % 4 and the same flip; inside a device rot and flip are 0.
All inputs are finite; a program needn't handle non-finite values.
Results may differ from a plain program's by a relative error of at most 0.0003.
Values sent between devices are 32-bit elements; how exact they have to be, the bound alone decides.
A program may use at most 64 MiB of HBM per device.

v0:
```python
import functools
import math

import jax
import jax.numpy as jnp
import ml_dtypes
import numpy as np
from jax import lax
from jax.experimental import pallas as pl
from jax.experimental.pallas import tpu as pltpu
from jax.sharding import PartitionSpec as P

TW = 8
LANES = 128

lift_gain = 10.0
step_size = 0.02
viscosity = 0.05
penalty = 2.0
section_a = -567301805773.0 / 1357537059087.0
section_b = 2404267990393.0 / 2016746695238.0

f32 = jnp.float32
bf16 = jnp.bfloat16


def build_derivative():
    points = np.array([-1.0, -math.sqrt(3.0 / 7.0), 0.0, math.sqrt(3.0 / 7.0), 1.0])
    weights = np.array(
        [
            1.0 / np.prod([points[row] - points[col] for col in range(5) if col != row])
            for row in range(5)
        ]
    )
    table = np.zeros((5, 5))
    for row in range(5):
        for col in range(5):
            if row != col:
                table[row, col] = weights[col] / weights[row] / (points[row] - points[col])
        table[row, row] = -np.sum(table[row])
    return table


def face_node(face, node):
    return [(4, node), (node, 4), (0, node), (node, 0)][face]


def split_const(table):
    high = table.astype(ml_dtypes.bfloat16)
    low = (table - high.astype(np.float64)).astype(ml_dtypes.bfloat16)
    return np.concatenate([high, low, high], axis=1)


def build_tables():
    d = build_derivative()
    eye = np.eye(5)
    dx = np.zeros((32, 32))
    dy = np.zeros((32, 32))
    dx[:25, :25] = np.kron(d, eye)
    dy[:25, :25] = np.kron(eye, d)
    pick = np.zeros((32, 32))
    for face in range(4):
        for node in range(5):
            a, b = face_node(face, node)
            pick[face * 8 + node, a * 5 + b] = 1.0
    normal_x = np.repeat([1.0, 0.0, -1.0, 0.0], 8)
    normal_y = np.repeat([0.0, 1.0, 0.0, -1.0], 8)
    lift_x = pick.T * normal_x[None] * (0.5 * lift_gain)
    lift_y = pick.T * normal_y[None] * (0.5 * lift_gain)
    grad_x = np.concatenate([dx, lift_x], axis=1)
    grad_y = np.concatenate([dy, lift_y], axis=1)
    grad = np.concatenate([grad_x, grad_y, pick @ grad_x, pick @ grad_y], axis=0)
    volume = np.concatenate([-dx, -dy, lift_gain * pick.T], axis=1)
    late = lift_gain * 0.5 * viscosity * pick.T
    out = np.zeros((224, 384), ml_dtypes.bfloat16)
    out[:128, :192] = split_const(grad)
    out[:128, 192:288] = split_const(grad[:, 32:])
    out[128:160, :288] = split_const(volume)
    out[160:192, :96] = split_const(late)
    out[192:224, :32] = pick.astype(ml_dtypes.bfloat16)
    out[192:224, 32:64] = pick.astype(ml_dtypes.bfloat16)
    return out


def halves(x):
    high = x.astype(bf16)
    low = (x - high.astype(f32)).astype(bf16)
    return high, low


def dot(a, b):
    return lax.dot_general(a, b, (((1,), (0,)), ((), ())), preferred_element_type=f32)


def dot_t(a, b):
    return lax.dot_general(a, b, (((1,), (1,)), ((), ())), preferred_element_type=f32)


def dot3(table, x):
    high, low = halves(x)
    return dot(table, jnp.concatenate([high, high, low], axis=0))


def onehot(mask):
    return jnp.where(mask, 1.0, 0.0).astype(bf16)


def permute(x, perm):
    rows = x.shape[0]
    high, low = halves(x)
    both = dot(jnp.concatenate([high, low], axis=0), perm)
    return both[:rows] + both[rows:]


def iota(shape, dim):
    return lax.broadcasted_iota(jnp.int32, shape, dim)


def kernel(
    plan,
    state_hbm,
    neighbor_hbm,
    neighbor_face_hbm,
    seam_hbm,
    tables_hbm,
    change,
    state,
    neighbor,
    neighbor_face,
    seam,
    tables,
    padded,
    sent,
    arrived,
    own_faces,
    early_grads,
    early_change,
    load_sem,
    send_sem,
    recv_sem,
):
    elems, levels, curve_count, strip_count, links, rows_of, offsets = plan
    columns = elems * levels
    inner = LANES // elems
    outer_levels = levels // inner
    groups = 4 * outer_levels
    span = 4 * LANES
    total_rows = offsets[-1] + rows_of[-1]
    link_count = len(links)
    link_rows = -(-link_count // 8) * 8

    curve_pos = lax.axis_index("curve")
    strip_pos = lax.axis_index("sub")
    device_pos = curve_pos * strip_count + strip_pos
    places = []
    for axis, step in links:
        if axis == "curve":
            places.append((lax.rem(curve_pos + step + curve_count, curve_count), strip_pos))
        else:
            places.append((curve_pos, lax.rem(strip_pos + step + strip_count, strip_count)))

    barrier = pltpu.get_barrier_semaphore()
    for place in places:
        pl.semaphore_signal(
            barrier, inc=1, device_id=place, device_id_type=pl.DeviceIdType.MESH
        )
    loads = [
        pltpu.make_async_copy(source_ref, target_ref, load_sem.at[index])
        for index, (source_ref, target_ref) in enumerate(
            [
                (neighbor_hbm, neighbor),
                (neighbor_face_hbm, neighbor_face),
                (seam_hbm, seam),
                (state_hbm, state),
                (tables_hbm, tables),
            ]
        )
    ]
    for load in loads:
        load.start()
    for load in loads[:3]:
        load.wait()

    def widen(ref):
        block = ref[...]
        return jnp.concatenate([block] * inner, axis=1)

    across = widen(neighbor)
    face_back = widen(neighbor_face)
    codes = widen(seam)
    owner = across // elems
    place_in = across % elems
    turn = codes % 4
    flipped = codes // 4
    sub_level = iota((4, LANES), 1) // elems
    position = face_back * LANES + sub_level * elems + place_in
    source = jnp.where(owner == device_pos, position, -1)
    heading = (face_back + turn) % 4
    cosine = jnp.where(turn == 0, 1.0, 0.0) - jnp.where(turn == 2, 1.0, 0.0)
    sine = jnp.where(turn == 3, 1.0, 0.0) - jnp.where(turn == 1, 1.0, 0.0)
    head_x = jnp.where(heading == 0, 1.0, 0.0) - jnp.where(heading == 2, 1.0, 0.0)
    head_y = jnp.where(heading == 1, 1.0, 0.0) - jnp.where(heading == 3, 1.0, 0.0)

    link_iota = iota((link_rows, LANES), 0)
    target = jnp.full((link_rows, LANES), -1, jnp.int32)
    base = jnp.zeros((link_rows, LANES), f32)
    for index, place in enumerate(places):
        target = jnp.where(link_iota == index, place[0] * strip_count + place[1], target)
        base = jnp.where(link_iota == index, float(offsets[index] + 1), base)
    base = base + (iota((link_rows, LANES), 1) // elems).astype(f32)
    member = [
        jnp.where(owner[face : face + 1] == target, 1.0, 0.0) for face in range(4)
    ]
    from_lane = iota((LANES, 2 * LANES), 0)
    to_lane = iota((LANES, 2 * LANES), 1)
    same = from_lane // elems == (to_lane % LANES) // elems
    earlier = same & ((from_lane < to_lane) | (to_lane >= LANES))
    counts = dot(jnp.concatenate(member, axis=0).astype(bf16), onehot(earlier))
    before = jnp.zeros((link_rows, LANES), f32)
    slot_rows = []
    for face in range(4):
        part = counts[face * link_rows : (face + 1) * link_rows]
        rank = part[:, :LANES] + before
        before = before + part[:, LANES:]
        slot_rows.append(
            jnp.sum(member[face] * (base + inner * rank), axis=0, keepdims=True)
        )
    slot_row = jnp.concatenate(slot_rows, axis=1)
    pack = onehot(
        (iota((total_rows, span), 0) + 1).astype(f32)
        == jnp.broadcast_to(slot_row, (total_rows, span))
    )
    pack2 = jnp.concatenate([pack, pack], axis=1)

    def local_table():
        span_iota = iota((span, LANES), 0)
        return jnp.concatenate(
            [onehot(span_iota == source[face : face + 1]) for face in range(4)], axis=1
        )

    meta_iota = iota((8, LANES), 0)
    meta_blocks = []
    for face in range(4):
        block = jnp.zeros((8, LANES), f32)
        for row, values in enumerate(
            [flipped.astype(f32), cosine, sine, (position + 1).astype(f32)]
        ):
            block = jnp.where(meta_iota == row, values[face : face + 1], block)
        meta_blocks.append(block)
    meta = jnp.concatenate(meta_blocks, axis=1)
    heads_x = jnp.concatenate(
        [jnp.broadcast_to(head_x[face : face + 1], (8, LANES)) for face in range(4)], axis=0
    )
    heads_y = jnp.concatenate(
        [jnp.broadcast_to(head_y[face : face + 1], (8, LANES)) for face in range(4)], axis=0
    )

    def to_exchange(faces):
        return jnp.concatenate(
            [
                jnp.concatenate(
                    [
                        faces[face * 8 : face * 8 + 8, group * LANES : (group + 1) * LANES]
                        for face in range(4)
                    ],
                    axis=1,
                )
                for group in range(groups)
            ],
            axis=0,
        )

    def from_exchange(block):
        return jnp.concatenate(
            [
                jnp.concatenate(
                    [
                        block[group * 8 : group * 8 + 8, face * LANES : (face + 1) * LANES]
                        for group in range(groups)
                    ],
                    axis=1,
                )
                for face in range(4)
            ],
            axis=0,
        )

    data_lanes = groups * 8
    field_lanes = outer_levels * 8
    lane = iota((total_rows, LANES), 1)
    node_lane = lane % 8
    in_data = lane < data_lanes

    def copy_of(turn_index, index):
        rows = pl.ds(offsets[index], rows_of[index])
        return pltpu.make_async_remote_copy(
            src_ref=sent.at[turn_index, rows],
            dst_ref=arrived.at[turn_index, rows],
            send_sem=send_sem.at[turn_index, index],
            recv_sem=recv_sem.at[turn_index, index],
            device_id=places[index],
            device_id_type=pl.DeviceIdType.MESH,
        )

    def post(turn_index, block, flags):
        if flags is None:
            pieces = [block, meta]
            if data_lanes + 8 < LANES:
                pieces.append(jnp.zeros((LANES - data_lanes - 8, span), f32))
            block = jnp.concatenate(pieces, axis=0)
        high, low = halves(block)
        message = dot_t(pack2, jnp.concatenate([high, low], axis=1))
        if flags is None:
            flags = [
                jnp.broadcast_to(
                    message[:, data_lanes + index : data_lanes + index + 1], message.shape
                )
                for index in range(3)
            ]
        else:
            rest = jnp.zeros((total_rows, LANES - data_lanes), f32)
            message = jnp.concatenate([message, rest], axis=1)
        flip, cos, sin = flags
        mirrored = message
        for node, shift in ((0, LANES - 4), (1, LANES - 2), (3, 2), (4, 4)):
            mirrored = jnp.where(
                node_lane == node, pltpu.roll(message, shift, axis=1), mirrored
            )
        aligned = jnp.where(in_data & (flip > 0.5), mirrored, message)
        field = lane // field_lanes
        turned_u = cos * aligned - sin * pltpu.roll(aligned, LANES - field_lanes, axis=1)
        turned_v = cos * aligned + sin * pltpu.roll(aligned, field_lanes, axis=1)
        aligned = jnp.where(field == 1, turned_u, jnp.where(field == 2, turned_v, aligned))
        sent[turn_index] = aligned
        if turn_index == 0:
            pl.semaphore_wait(barrier, link_count)
        for index in range(link_count):
            copy_of(turn_index, index).start()
        return flags

    def gather_local(block):
        rows = block.shape[0]
        high, low = halves(block)
        both = dot(jnp.concatenate([high, low], axis=0), local_table())
        return both[:rows] + both[rows:]

    def await_all(turn_index):
        for index in range(link_count):
            copy_of(turn_index, index).wait_recv()

    def spread_table():
        message = arrived[0]
        spot = jnp.broadcast_to(
            message[:, data_lanes + 3 : data_lanes + 4], (total_rows, span)
        )
        return onehot((iota((total_rows, span), 1) + 1).astype(f32) == spot)

    def collect(turn_index, spread):
        message = arrived[turn_index]
        high, low = halves(jnp.transpose(message)[:data_lanes])
        both = dot(jnp.concatenate([high, low], axis=0), spread)
        return both[:data_lanes] + both[data_lanes:]

    row = iota((columns, columns), 0)
    col = iota((columns, columns), 1)
    to_level = onehot(row == (col % elems) * levels + col // elems)
    to_elem = onehot(row == (col % levels) * elems + col // levels)

    padded[...] = jnp.zeros_like(padded)
    for load in loads[3:]:
        load.wait()
    for field in range(4):
        padded[field, :25] = state[:, field, :]
    nodal = permute(padded[...].reshape(128, columns), to_level)
    values = jnp.concatenate(
        [nodal[field * 32 : field * 32 + 32] for field in range(4)], axis=1
    )
    high, low = halves(values)
    faces_in = dot(tables[192:224, :64], jnp.concatenate([high, low], axis=0))

    def fields_of(wide):
        return [wide[:, field * columns : (field + 1) * columns] for field in range(4)]

    def elementwise_lanes(wide):
        return permute(jnp.concatenate(fields_of(wide), axis=0), to_elem)

    def early_part(values, faces_in, faces_out, grad_x, grad_y, face_gx, face_gy, own_slope):
        face_of_row = iota((32, columns), 0) // 8
        normal_x = jnp.where(face_of_row == 0, 1.0, 0.0) - jnp.where(face_of_row == 2, 1.0, 0.0)
        normal_y = jnp.where(face_of_row == 1, 1.0, 0.0) - jnp.where(face_of_row == 3, 1.0, 0.0)

        def flux_of(faces):
            speed = faces[1] * normal_x + faces[2] * normal_y
            return [speed, faces[0] * normal_x, faces[0] * normal_y, faces[3] * speed], speed

        inside, outside = fields_of(faces_in), fields_of(faces_out)
        gx_in, gy_in = fields_of(face_gx), fields_of(face_gy)
        slope_own = fields_of(own_slope)
        flux_in, speed_in = flux_of(inside)
        flux_out, speed_out = flux_of(outside)
        wave = 1.0 + jnp.maximum(jnp.abs(speed_in), jnp.abs(speed_out))
        terms = []
        for field in range(4):
            slope_in = gx_in[field] * normal_x + gy_in[field] * normal_y
            jump = outside[field] - inside[field]
            terms.append(
                0.5 * (flux_in[field] - flux_out[field])
                - 0.5 * viscosity * (slope_in - slope_own[field])
                + (0.5 * wave + viscosity * penalty) * jump
            )
        face_term = jnp.concatenate(terms, axis=1)
        pressure, vel_u, vel_v, theta = fields_of(values)
        nothing = jnp.zeros_like(pressure)
        flux_x = jnp.concatenate([vel_u, pressure, nothing, theta * vel_u], axis=1)
        flux_y = jnp.concatenate([vel_v, nothing, pressure, theta * vel_v], axis=1)
        tendency = dot3(
            tables[128:160, :288],
            jnp.concatenate(
                [flux_x - viscosity * grad_x, flux_y - viscosity * grad_y, face_term], axis=0
            ),
        )

        return elementwise_lanes(tendency)

    block_in = to_exchange(faces_in)
    flags = post(0, block_in, None)
    always = device_pos >= 0

    @pl.when(always)
    def _():
        own = from_exchange(gather_local(block_in))
        own_faces[...] = own
        early_grads[...] = dot3(
            tables[:128, :192], jnp.concatenate([values, own - faces_in], axis=0)
        )

    await_all(0)
    spread = spread_table()
    far_faces = from_exchange(collect(0, spread))
    face_grads = early_grads[64:128] + dot3(tables[64:128, 192:288], far_faces)
    face_gx, face_gy = face_grads[:32], face_grads[32:]
    wide_x = jnp.concatenate([heads_x] * groups, axis=1)
    wide_y = jnp.concatenate([heads_y] * groups, axis=1)
    block_grad = to_exchange(face_gx * wide_x + face_gy * wide_y)
    post(1, block_grad, flags)

    @pl.when(always)
    def _():
        own_slope = from_exchange(gather_local(block_grad))
        grads = early_grads[:64] + dot3(tables[:64, 192:288], far_faces)
        faces_out = own_faces[...] + far_faces
        grad_x, grad_y = grads[:32], grads[32:]
        early_change[...] = early_part(
            values, faces_in, faces_out, grad_x, grad_y, face_gx, face_gy, own_slope
        )

    await_all(1)
    far_slope = from_exchange(collect(1, spread))
    late = elementwise_lanes(dot3(tables[160:192, :96], far_slope))
    total = early_change[...] + late
    for field in range(4):
        change[:, field, :] = step_size * total[field * 32 : field * 32 + 25]

    for turn_index in range(2):
        for index in range(link_count):
            copy_of(turn_index, index).wait_send()


def body(curve_count, strip_count, state, register, neighbor, neighbor_face, seam):
    elems = neighbor.shape[1]
    levels = state.shape[2] // elems
    inner = LANES // elems
    reach = min(7, (curve_count - 1) // 2)
    slots = (TW + reach - 1) // reach
    links, rows_of = [], []
    for distance in range(reach, 0, -1):
        for direction in (1, -1):
            links.append(("curve", direction * distance))
            rows_of.append(-(-slots * inner // 8) * 8)
    for direction in (1, -1):
        links.append(("sub", direction))
        rows_of.append(-(-TW * inner // 8) * 8)
    offsets = [sum(rows_of[:index]) for index in range(len(links))]
    total_rows = sum(rows_of)
    plan = (elems, levels, curve_count, strip_count, links, rows_of, offsets)
    vmem = pl.BlockSpec(memory_space=pltpu.VMEM)
    nodes_first = jnp.transpose(state, (1, 0, 2))
    change = pl.pallas_call(
        functools.partial(kernel, plan),
        out_shape=jax.ShapeDtypeStruct(nodes_first.shape, f32),
        in_specs=[pl.BlockSpec(memory_space=pl.ANY)] * 5,
        out_specs=vmem,
        scratch_shapes=[
            pltpu.VMEM(nodes_first.shape, f32),
            pltpu.VMEM(neighbor.shape, jnp.int32),
            pltpu.VMEM(neighbor.shape, jnp.int32),
            pltpu.VMEM(neighbor.shape, jnp.int32),
            pltpu.VMEM((224, 384), bf16),
            pltpu.VMEM((4, 32, state.shape[2]), f32),
            pltpu.VMEM((2, total_rows, LANES), f32),
            pltpu.VMEM((2, total_rows, LANES), f32),
            pltpu.VMEM((32, 4 * state.shape[2]), f32),
            pltpu.VMEM((128, 4 * state.shape[2]), f32),
            pltpu.VMEM((128, state.shape[2]), f32),
            pltpu.SemaphoreType.DMA((5,)),
            pltpu.SemaphoreType.DMA((2, len(links))),
            pltpu.SemaphoreType.DMA((2, len(links))),
        ],
        compiler_params=pltpu.CompilerParams(collective_id=0, has_side_effects=True),
    )(nodes_first, neighbor, neighbor_face, seam, jnp.asarray(build_tables()))
    next_register = section_a * register + jnp.transpose(change, (1, 0, 2))
    return state + section_b * next_register, next_register


def solution(mesh):
    wide = P(None, None, ("curve", "sub"))
    flat = P(None, ("curve", "sub"))
    return jax.shard_map(
        functools.partial(body, mesh.shape["curve"], mesh.shape["sub"]),
        mesh=mesh,
        in_specs=(wide, wide, flat, flat, flat),
        out_specs=(wide, wide),
        check_vma=False,
    )
```

profile of v0, /device:TPU:0, one launch (start us, length us, event | category | flops | bytes accessed | tf_op | source)
XLA Modules:
  0.0 19.0 jit_solution(2258992545023627555)
XLA Ops:
  0.6 0.0 copy-start
  0.6 0.0 copy-start.1
  0.7 16.7 %shard_map.77 = f32[25,4,256]{2,1,0:T(4,128)} custom-call(f32[25,4,256]{2,1,0:T(4,128)} %bitcast.4, s32[4,64]{1,0:T(4,128)} %neighbor_hbm.1, s32[4,64]{1,0:T(4,128)} %neighbor_face_hbm.1, s32[4,64]{1,0:T(4,128)} %seam_hbm.1, bf16[224,384]{1,0:T(8,128)(2,1)} %constant.6.clone.tables_hbm), custom_call_target="tpu_custom_call" | custom-call | tf_op jit(solution)/shard_map/pallas_call | solution.py:488
  17.3 0.0 copy-done
  17.3 0.0 copy-done.1
  17.3 1.6 %multiply_add_fusion = (f32[4,25,256]{2,0,1:T(4,128)}, f32[4,25,256]{2,0,1:T(4,128)}) fusion(f32[4,25,256]{2,0,1:T(4,128)S(1)} %copy-done, f32[25,4,256]{2,1,0:T(4,128)} %shard_map.77, f32[4,25,256]{2,0,1:T(4,128)S(1)} %copy-done.1), kind=kLoop, calls=%fused_computation.1 | loop fusion | flops 102400 | bytes 512000 | tf_op jit(solution)/shard_map/add | solution.py:512
Async XLA Ops:
  0.6 16.7 %copy-start = (f32[4,25,256]{2,0,1:T(4,128)S(1)}, f32[4,25,256]{2,0,1:T(4,128)}, u32[]{:S(2)}) copy-start(f32[4,25,256]{2,0,1:T(4,128)} %param.6) | copy-start | bytes 307204
  0.6 16.7 %copy-start.1 = (f32[4,25,256]{2,0,1:T(4,128)S(1)}, f32[4,25,256]{2,0,1:T(4,128)}, u32[]{:S(2)}) copy-start(f32[4,25,256]{2,0,1:T(4,128)} %param.7) | copy-start | bytes 307204
where the time goes:
time: 19.1 us; the launch traced here: 19 us
  Pallas kernels  16.7 us (87%)
  other arithmetic  1.63 us (9%)
  between operations  0.67 us (4%)
    pallas_call x1, Pallas kernels, body(): pl.pallas_call(functools.partial(kernel, plan), out_shape=jax.ShapeDtypeS...  16.7 us
    add x1, other arithmetic, body(): return (state + section_b * next_register, next_register)  1.63 us

commit v1 on v0

--- a/solution.py
+++ b/solution.py
@@ -485,9 +485,10 @@
     plan = (elems, levels, curve_count, strip_count, links, rows_of, offsets)
     vmem = pl.BlockSpec(memory_space=pltpu.VMEM)
     nodes_first = jnp.transpose(state, (1, 0, 2))
+    operands = (nodes_first, neighbor, neighbor_face, seam, jnp.asarray(build_tables()))
     change = pl.pallas_call(
         functools.partial(kernel, plan),
-        out_shape=jax.ShapeDtypeStruct(nodes_first.shape, f32),
+        out_shape=pltpu.VMEM(nodes_first.shape, f32),
         in_specs=[pl.BlockSpec(memory_space=pl.ANY)] * 5,
         out_specs=vmem,
         scratch_shapes=[
@@ -507,7 +508,7 @@
             pltpu.SemaphoreType.DMA((2, len(links))),
         ],
         compiler_params=pltpu.CompilerParams(collective_id=0, has_side_effects=True),
-    )(nodes_first, neighbor, neighbor_face, seam, jnp.asarray(build_tables()))
+    )(*[pltpu.with_memory_space_constraint(operand, pltpu.HBM) for operand in operands])
     next_register = section_a * register + jnp.transpose(change, (1, 0, 2))
     return state + section_b * next_register, next_register
 

time: 19.1 us -> 17.6 us (0.921)
  other arithmetic: 1.63 us -> 0.74 us
  Pallas kernels: 16.7 us -> 16 us
    add x1, other arithmetic: 1.63 us -> 0.74 us  [body(): return (state + section_b * next_register, next_register)]
    pallas_call x1, Pallas kernels: 16.7 us -> 16 us  [body(): pl.pallas_call(functools.partial(kernel, plan), out_shape=pltpu.VMEM(node...]
where the time goes in v1:
time: 17.6 us; the launch traced here: 17.4 us
  Pallas kernels  16 us (91%)
  other arithmetic  0.74 us (4%)
  between operations  0.67 us (4%)
    pallas_call x1, Pallas kernels, body(): pl.pallas_call(functools.partial(kernel, plan), out_shape=pltpu.VMEM(node...  16 us
    add x1, other arithmetic, body(): return (state + section_b * next_register, next_register)  0.74 us

profile of v1, /device:TPU:0, one launch (start us, length us, event | category | flops | bytes accessed | tf_op | source)
XLA Modules:
  0.0 17.4 jit_solution(4098973118807820457)
XLA Ops:
  0.6 0.0 copy-start
  0.6 0.0 copy-start.1
  0.7 16.0 %shard_map.77 = f32[25,4,256]{2,1,0:T(4,128)S(1)} custom-call(f32[25,4,256]{2,1,0:T(4,128)} %bitcast.4, s32[4,64]{1,0:T(4,128)} %neighbor_hbm.1, s32[4,64]{1,0:T(4,128)} %neighbor_face_hbm.1, s32[4,64]{1,0:T(4,128)} %seam_hbm.1, bf16[224,384]{1,0:T(8,128)(2,1)} %constant.6.clone.tables_hbm), custom_call_target="tpu_custom_call" | custom-call | tf_op jit(solution)/shard_map/pallas_call | solution.py:489
  16.7 0.0 copy-done
  16.7 0.0 copy-done.1
  16.7 0.7 %multiply_add_fusion = (f32[4,25,256]{2,0,1:T(4,128)}, f32[4,25,256]{2,0,1:T(4,128)}) fusion(f32[4,25,256]{2,0,1:T(4,128)S(1)} %copy-done, f32[25,4,256]{2,1,0:T(4,128)S(1)} %shard_map.77, f32[4,25,256]{2,0,1:T(4,128)S(1)} %copy-done.1), kind=kLoop, calls=%fused_computation.1 | loop fusion | flops 102400 | bytes 512000 | tf_op jit(solution)/shard_map/add | solution.py:513
Async XLA Ops:
  0.6 16.1 %copy-start = (f32[4,25,256]{2,0,1:T(4,128)S(1)}, f32[4,25,256]{2,0,1:T(4,128)}, u32[]{:S(2)}) copy-start(f32[4,25,256]{2,0,1:T(4,128)} %param.6) | copy-start | bytes 307204
  0.6 16.1 %copy-start.1 = (f32[4,25,256]{2,0,1:T(4,128)S(1)}, f32[4,25,256]{2,0,1:T(4,128)}, u32[]{:S(2)}) copy-start(f32[4,25,256]{2,0,1:T(4,128)} %param.7) | copy-start | bytes 307204

commit v2 on v0

--- a/solution.py
+++ b/solution.py
@@ -12,6 +12,7 @@
 
 TW = 8
 LANES = 128
+DIRECT_LIMIT = 64
 
 lift_gain = 10.0
 step_size = 0.02
@@ -51,7 +52,7 @@
     return np.concatenate([high, low, high], axis=1)
 
 
-def build_tables():
+def element_tables():
     d = build_derivative()
     eye = np.eye(5)
     dx = np.zeros((32, 32))
@@ -67,6 +68,11 @@
     normal_y = np.repeat([0.0, 1.0, 0.0, -1.0], 8)
     lift_x = pick.T * normal_x[None] * (0.5 * lift_gain)
     lift_y = pick.T * normal_y[None] * (0.5 * lift_gain)
+    return dx, dy, pick, normal_x, normal_y, lift_x, lift_y
+
+
+def build_tables():
+    dx, dy, pick, _, _, lift_x, lift_y = element_tables()
     grad_x = np.concatenate([dx, lift_x], axis=1)
     grad_y = np.concatenate([dy, lift_y], axis=1)
     grad = np.concatenate([grad_x, grad_y, pick @ grad_x, pick @ grad_y], axis=0)
@@ -82,6 +88,19 @@
     return out
 
 
+def build_direct_tables():
+    dx, dy, pick, normal_x, normal_y, lift_x, lift_y = element_tables()
+    slope = normal_x[:, None] * (pick @ dx) + normal_y[:, None] * (pick @ dy)
+    base = np.concatenate([-dx, -dy, viscosity * (dx @ dx + dy @ dy)], axis=1)
+    jump = viscosity * (dx @ lift_x + dy @ lift_y)
+    late = np.concatenate([lift_gain * pick.T, jump], axis=1)
+    out = np.zeros((128, 384), ml_dtypes.bfloat16)
+    out[:64, :96] = split_const(np.concatenate([pick, slope], axis=0))
+    out[64:96, :288] = split_const(base)
+    out[96:128, :192] = split_const(late)
+    return out
+
+
 def halves(x):
     high = x.astype(bf16)
     low = (x - high.astype(f32)).astype(bf16)
@@ -116,7 +135,7 @@
     return lax.broadcasted_iota(jnp.int32, shape, dim)
 
 
-def kernel(
+def two_round_kernel(
     plan,
     state_hbm,
     neighbor_hbm,
@@ -459,17 +478,383 @@
     late = elementwise_lanes(dot3(tables[160:192, :96], far_slope))
     total = early_change[...] + late
     for field in range(4):
-        change[:, field, :] = step_size * total[field * 32 : field * 32 + 25]
+        change[:, field, :] = total[field * 32 : field * 32 + 25]
 
     for turn_index in range(2):
         for index in range(link_count):
             copy_of(turn_index, index).wait_send()
 
 
+def direct_kernel(
+    plan,
+    state_hbm,
+    neighbor_hbm,
+    neighbor_face_hbm,
+    seam_hbm,
+    tables_hbm,
+    change,
+    sideways,
+    state,
+    neighbor,
+    neighbor_face,
+    seam,
+    tables,
+    padded,
+    sent,
+    arrived,
+    notice,
+    notices,
+    spread,
+    known,
+    base_change,
+    load_sem,
+    send_sem,
+    recv_sem,
+    notice_send_sem,
+    notice_recv_sem,
+):
+    elems, levels, curve_count, strip_count, links, rows_of, offsets = plan
+    columns = elems * levels
+    span = 4 * columns
+    inner = LANES // elems
+    outer_levels = levels // inner
+    total_rows = offsets[-1] + rows_of[-1]
+    link_count = len(links)
+    link_rows = -(-link_count // 8) * 8
+    half = LANES // outer_levels
+
+    curve_pos = lax.axis_index("curve")
+    strip_pos = lax.axis_index("sub")
+    device_pos = curve_pos * strip_count + strip_pos
+
+    def place_at(curve_step, strip_step):
+        return (
+            lax.rem(curve_pos + curve_step + curve_count, curve_count),
+            lax.rem(strip_pos + strip_step + strip_count, strip_count),
+        )
+
+    places = [place_at(step, 0) if axis == "curve" else place_at(0, step) for axis, step in links]
+    others = [
+        place_at(curve_step, strip_step)
+        for curve_step in range(curve_count)
+        for strip_step in range(strip_count)
+        if curve_step or strip_step
+    ]
+
+    barrier = pltpu.get_barrier_semaphore()
+    for place in others:
+        pl.semaphore_signal(
+            barrier, inc=1, device_id=place, device_id_type=pl.DeviceIdType.MESH
+        )
+    loads = [
+        pltpu.make_async_copy(source_ref, target_ref, load_sem.at[index])
+        for index, (source_ref, target_ref) in enumerate(
+            [
+                (neighbor_hbm, neighbor),
+                (neighbor_face_hbm, neighbor_face),
+                (seam_hbm, seam),
+                (state_hbm, state),
+                (tables_hbm, tables),
+            ]
+        )
+    ]
+    for load in loads:
+        load.start()
+    padded[...] = jnp.zeros_like(padded)
+
+    def copy_of(index):
+        rows = pl.ds(offsets[index], rows_of[index])
+        return pltpu.make_async_remote_copy(
+            src_ref=sent.at[rows],
+            dst_ref=arrived.at[rows],
+            send_sem=send_sem.at[index],
+            recv_sem=recv_sem.at[index],
+            device_id=places[index],
+            device_id_type=pl.DeviceIdType.MESH,
+        )
+
+    def notice_of(index):
+        return pltpu.make_async_remote_copy(
+            src_ref=notice.at[pl.ds(0, 1)],
+            dst_ref=notices.at[pl.ds(index, 1)],
+            send_sem=notice_send_sem.at[index],
+            recv_sem=notice_recv_sem.at[index],
+            device_id=others[index],
+            device_id_type=pl.DeviceIdType.MESH,
+        )
+
+    for load in loads[:3]:
+        load.wait()
+
+    def widen(ref):
+        block = ref[...]
+        return jnp.concatenate([block] * inner, axis=1)
+
+    across = widen(neighbor)
+    face_back = widen(neighbor_face)
+    codes = widen(seam)
+    owner = across // elems
+    place_in = across % elems
+    turn = codes % 4
+    flipped = codes // 4
+    own_face = iota((4, LANES), 0)
+    quarter = (face_back + turn - own_face + 4) % 4
+    odd = jnp.where(quarter % 2 == 1, 1.0, 0.0)
+    notice[...] = jnp.broadcast_to(jnp.sum(odd, axis=0, keepdims=True), (8, LANES))
+    side = jnp.where(quarter == 0, 1.0, -1.0)
+    cosine = jnp.where(turn == 0, 1.0, 0.0) - jnp.where(turn == 2, 1.0, 0.0)
+    sine = jnp.where(turn == 3, 1.0, 0.0) - jnp.where(turn == 1, 1.0, 0.0)
+
+    link_iota = iota((link_rows, LANES), 0)
+    target = jnp.full((link_rows, LANES), -1, jnp.int32)
+    base = jnp.zeros((link_rows, LANES), f32)
+    base_back = jnp.zeros((link_rows, LANES), f32)
+    for index, place in enumerate(places):
+        here = link_iota == index
+        target = jnp.where(here, place[0] * strip_count + place[1], target)
+        base = jnp.where(here, float(offsets[index] + 1), base)
+        base_back = jnp.where(here, float(offsets[index ^ 1] + 1), base_back)
+    member = [
+        jnp.where(owner[face : face + 1] == target, 1.0, 0.0) for face in range(4)
+    ]
+    from_lane = iota((LANES, 2 * LANES), 0)
+    to_lane = iota((LANES, 2 * LANES), 1)
+    same = from_lane // elems == (to_lane % LANES) // elems
+    earlier = same & ((from_lane < to_lane) | (to_lane >= LANES))
+    counts = dot(jnp.concatenate(member, axis=0).astype(bf16), onehot(earlier))
+    before = jnp.zeros((link_rows, LANES), f32)
+    slot_rows = []
+    for face in range(4):
+        part = counts[face * link_rows : (face + 1) * link_rows]
+        rank = part[:, :LANES] + before
+        before = before + part[:, LANES:]
+        slot_rows.append(
+            jnp.sum(member[face] * (base + inner * rank), axis=0, keepdims=True)
+        )
+
+    stretch = onehot(iota((LANES, columns), 0) == iota((LANES, columns), 1) // levels)
+
+    def stretched(per_face):
+        rows = []
+        for values in per_face:
+            rows.append(values)
+            rows.append(jnp.zeros_like(values))
+        wide = dot(jnp.concatenate(rows, axis=0).astype(bf16), stretch)
+        return [wide[8 * index : 8 * index + 8] for index in range(len(per_face))]
+
+    slot, flip_wide, cos_wide, sin_wide, side_wide = stretched(
+        [jnp.concatenate(slot_rows, axis=0), flipped.astype(f32), cosine, sine, side]
+    )
+    level = iota((8, columns), 1) % levels
+
+    def rows_for(slot, stride):
+        spot = slot + (level % inner + level // inner * stride).astype(f32)
+        return jnp.where(slot > 0.5, spot, 0.0)
+
+    def hot_rows(count, spots):
+        count_iota = (iota((count, columns), 0) + 1).astype(f32)
+        return jnp.concatenate(
+            [
+                onehot(
+                    count_iota == jnp.broadcast_to(spots[face : face + 1], (count, columns))
+                )
+                for face in range(4)
+            ],
+            axis=1,
+        )
+
+    pack = hot_rows(outer_levels * total_rows, rows_for(slot, total_rows))
+
+    def over_faces(wide, rows):
+        return jnp.concatenate(
+            [jnp.broadcast_to(wide[face : face + 1], (rows, columns)) for face in range(4)],
+            axis=1,
+        )
+
+    def to_fields(block):
+        return jnp.concatenate(
+            [
+                jnp.concatenate(
+                    [
+                        block[face * 8 : face * 8 + 8, field * columns : (field + 1) * columns]
+                        for face in range(4)
+                    ],
+                    axis=1,
+                )
+                for field in range(4)
+            ],
+            axis=0,
+        )
+
+    def to_faces(block):
+        return jnp.concatenate(
+            [
+                jnp.concatenate(
+                    [
+                        block[field * 8 : field * 8 + 8, face * columns : (face + 1) * columns]
+                        for field in range(4)
+                    ],
+                    axis=1,
+                )
+                for face in range(4)
+            ],
+            axis=0,
+        )
+
+    for load in loads[3:]:
+        load.wait()
+    for field in range(4):
+        padded[field, :25] = state[:, field, :]
+    values = jnp.concatenate([padded[field] for field in range(4)], axis=1)
+    on_faces = dot3(tables[:64, :96], values)
+    traces = to_fields(on_faces[:32])
+    slopes = to_fields(on_faces[32:])
+    row32 = iota((32, span), 0)
+    marked = jnp.where(row32 == 5, over_faces(flip_wide, 32), traces)
+    marked = jnp.where(row32 == 13, over_faces(cos_wide, 32), marked)
+    marked = jnp.where(row32 == 21, over_faces(sin_wide, 32), marked)
+    slopes_out = slopes * over_faces(side_wide, 32)
+    high, low = halves(jnp.concatenate([marked, slopes_out], axis=0))
+    stacked = dot_t(pack, jnp.concatenate([high, low], axis=0))
+    lane = iota((total_rows, LANES), 1)
+    message = jnp.zeros((total_rows, LANES), f32)
+    for index in range(outer_levels):
+        part = stacked[index * total_rows : (index + 1) * total_rows]
+        part = part + pltpu.roll(part, half, axis=1)
+        message = jnp.where(lane // half == index, part, message)
+    flip, cos, sin = [
+        jnp.broadcast_to(message[:, spot : spot + 1], message.shape) for spot in (5, 13, 21)
+    ]
+    node_lane = lane % 8
+    field_lane = lane % 32 // 8
+    mirrored = message
+    for node, shift in ((0, LANES - 4), (1, LANES - 2), (3, 2), (4, 4)):
+        mirrored = jnp.where(node_lane == node, pltpu.roll(message, shift, axis=1), mirrored)
+    aligned = jnp.where(flip > 0.5, mirrored, message)
+    turned_u = cos * aligned - sin * pltpu.roll(aligned, LANES - 8, axis=1)
+    turned_v = cos * aligned + sin * pltpu.roll(aligned, 8, axis=1)
+    sent[...] = jnp.where(
+        field_lane == 1, turned_u, jnp.where(field_lane == 2, turned_v, aligned)
+    )
+    pl.semaphore_wait(barrier, len(others))
+    for index in range(link_count):
+        copy_of(index).start()
+    for index in range(len(others)):
+        notice_of(index).start()
+    always = device_pos >= 0
+
+    @pl.when(always)
+    def _():
+        first_of = owner * (4 * elems)
+        key = (first_of + face_back * elems + place_in).astype(f32)
+        first_of = first_of.astype(f32)
+        key_down = jnp.transpose(jnp.concatenate([key, key], axis=0))
+        back_rows = []
+        for face in range(4):
+            smaller = jnp.zeros((elems, LANES), f32)
+            for other in range(4):
+                rival = jnp.broadcast_to(key_down[:elems, other : other + 1], (elems, LANES))
+                mine = (rival < key[face : face + 1]) & (rival >= first_of[face : face + 1])
+                smaller = smaller + jnp.where(mine, 1.0, 0.0)
+            rank = jnp.sum(smaller, axis=0, keepdims=True)
+            back_rows.append(
+                jnp.sum(member[face] * (base_back + inner * rank), axis=0, keepdims=True)
+            )
+        at_home = owner == device_pos
+        homes = [
+            jnp.where(at_home & (face_back == face), place_in + 1, 0).astype(f32)
+            for face in range(4)
+        ]
+        back, *homes = stretched([jnp.concatenate(back_rows, axis=0)] + homes)
+        spread[...] = hot_rows(outer_levels * LANES, rows_for(back, LANES))
+
+        both_high, both_low = halves(jnp.concatenate([traces, slopes_out], axis=0))
+        both = jnp.concatenate([both_high, both_low], axis=0)
+        found = jnp.zeros((128, span), f32)
+        for face in range(4):
+            spots = jnp.where(
+                homes[face] > 0.5, homes[face] * levels + (level - levels + 1).astype(f32), 0.0
+            )
+            found = found + dot(
+                both[:, face * columns : (face + 1) * columns], hot_rows(columns, spots)
+            )
+        found = found[:64] + found[64:]
+        known[:32] = traces
+        known[32:64] = found[:32]
+        known[64:96] = found[32:] - slopes
+        known[96:128] = over_faces(
+            0.5 + viscosity * penalty - 0.25 * lift_gain * viscosity * (1.0 + side_wide), 32
+        )
+        pressure, vel_u, vel_v, theta = [
+            values[:, field * columns : (field + 1) * columns] for field in range(4)
+        ]
+        nothing = jnp.zeros_like(pressure)
+        flux_x = jnp.concatenate([vel_u, pressure, nothing, theta * vel_u], axis=1)
+        flux_y = jnp.concatenate([vel_v, nothing, pressure, theta * vel_v], axis=1)
+        base_change[...] = dot3(
+            tables[64:96, :288], jnp.concatenate([flux_x, flux_y, values], axis=0)
+        )
+
+    for index in range(link_count):
+        copy_of(index).wait_recv()
+    filler = jnp.zeros((LANES - total_rows, LANES), f32)
+    turned = jnp.transpose(jnp.concatenate([arrived[...], filler], axis=0))
+    turned = jnp.concatenate(
+        [turned[half * index : half * (index + 1)] for index in range(outer_levels)], axis=1
+    )
+    high, low = halves(turned)
+    far = dot(jnp.concatenate([high, low], axis=0), spread[...])
+    far = far[:half] + far[half:]
+    inside = known[:32]
+    outside = known[32:64] + far[:32]
+    jump = outside - inside
+    slope_term = (0.5 * viscosity) * (known[64:96] + far[32:])
+    weight = known[96:128]
+    terms = []
+    for face in range(4):
+        sides = slice(face * columns, (face + 1) * columns)
+        ins = [inside[field * 8 : field * 8 + 8, sides] for field in range(4)]
+        outs = [outside[field * 8 : field * 8 + 8, sides] for field in range(4)]
+        step = [jump[field * 8 : field * 8 + 8, sides] for field in range(4)]
+        normal = 1 + face % 2
+        sign = 1.0 if face < 2 else -1.0
+        raw_in, raw_out = ins[normal], outs[normal]
+        wave = weight[:8, sides] + 0.5 * jnp.maximum(jnp.abs(raw_in), jnp.abs(raw_out))
+        drops = [
+            (-0.5 * sign) * step[normal],
+            None,
+            None,
+            (0.5 * sign) * (ins[3] * raw_in - outs[3] * raw_out),
+        ]
+        drops[normal] = (-0.5 * sign) * step[0]
+        rows = []
+        for field in range(4):
+            term = wave * step[field] + slope_term[field * 8 : field * 8 + 8, sides]
+            rows.append(term if drops[field] is None else term + drops[field])
+        terms.append(jnp.concatenate(rows, axis=0))
+    face_term = jnp.concatenate(terms, axis=1)
+    total = base_change[...] + dot3(
+        tables[96:128, :192], jnp.concatenate([to_faces(face_term), to_faces(jump)], axis=0)
+    )
+    for field in range(4):
+        change[:, field, :] = total[:25, field * columns : (field + 1) * columns]
+
+    for index in range(len(others)):
+        notice_of(index).wait_recv()
+    heard = jnp.max(notices[: len(others)]) + jnp.max(notice[...])
+    sideways[0] = jnp.where(heard > 0.5, 1, 0)
+    for index in range(link_count):
+        copy_of(index).wait_send()
+    for index in range(len(others)):
+        notice_of(index).wait_send()
+
+
 def body(curve_count, strip_count, state, register, neighbor, neighbor_face, seam):
     elems = neighbor.shape[1]
-    levels = state.shape[2] // elems
+    columns = state.shape[2]
+    levels = columns // elems
     inner = LANES // elems
+    outer_levels = levels // inner
     reach = min(7, (curve_count - 1) // 2)
     slots = (TW + reach - 1) // reach
     links, rows_of = [], []
@@ -485,30 +870,74 @@
     plan = (elems, levels, curve_count, strip_count, links, rows_of, offsets)
     vmem = pl.BlockSpec(memory_space=pltpu.VMEM)
     nodes_first = jnp.transpose(state, (1, 0, 2))
-    change = pl.pallas_call(
-        functools.partial(kernel, plan),
-        out_shape=jax.ShapeDtypeStruct(nodes_first.shape, f32),
-        in_specs=[pl.BlockSpec(memory_space=pl.ANY)] * 5,
-        out_specs=vmem,
-        scratch_shapes=[
+
+    def call(kernel, tables, outputs, out_specs, scratch, collective_id):
+        operands = (nodes_first, neighbor, neighbor_face, seam, jnp.asarray(tables))
+        return pl.pallas_call(
+            functools.partial(kernel, plan),
+            out_shape=outputs,
+            in_specs=[pl.BlockSpec(memory_space=pl.ANY)] * 5,
+            out_specs=out_specs,
+            scratch_shapes=[
+                pltpu.VMEM(nodes_first.shape, f32),
+                pltpu.VMEM(neighbor.shape, jnp.int32),
+                pltpu.VMEM(neighbor.shape, jnp.int32),
+                pltpu.VMEM(neighbor.shape, jnp.int32),
+                pltpu.VMEM(tables.shape, bf16),
+                pltpu.VMEM((4, 32, columns), f32),
+            ]
+            + scratch,
+            compiler_params=pltpu.CompilerParams(
+                collective_id=collective_id, has_side_effects=True
+            ),
+        )(*[pltpu.with_memory_space_constraint(operand, pltpu.HBM) for operand in operands])
+
+    def two_rounds():
+        return call(
+            two_round_kernel,
+            build_tables(),
             pltpu.VMEM(nodes_first.shape, f32),
-            pltpu.VMEM(neighbor.shape, jnp.int32),
-            pltpu.VMEM(neighbor.shape, jnp.int32),
-            pltpu.VMEM(neighbor.shape, jnp.int32),
-            pltpu.VMEM((224, 384), bf16),
-            pltpu.VMEM((4, 32, state.shape[2]), f32),
-            pltpu.VMEM((2, total_rows, LANES), f32),
-            pltpu.VMEM((2, total_rows, LANES), f32),
-            pltpu.VMEM((32, 4 * state.shape[2]), f32),
-            pltpu.VMEM((128, 4 * state.shape[2]), f32),
-            pltpu.VMEM((128, state.shape[2]), f32),
-            pltpu.SemaphoreType.DMA((5,)),
-            pltpu.SemaphoreType.DMA((2, len(links))),
-            pltpu.SemaphoreType.DMA((2, len(links))),
-        ],
-        compiler_params=pltpu.CompilerParams(collective_id=0, has_side_effects=True),
-    )(nodes_first, neighbor, neighbor_face, seam, jnp.asarray(build_tables()))
-    next_register = section_a * register + jnp.transpose(change, (1, 0, 2))
+            vmem,
+            [
+                pltpu.VMEM((2, total_rows, LANES), f32),
+                pltpu.VMEM((2, total_rows, LANES), f32),
+                pltpu.VMEM((32, 4 * columns), f32),
+                pltpu.VMEM((128, 4 * columns), f32),
+                pltpu.VMEM((128, columns), f32),
+                pltpu.SemaphoreType.DMA((5,)),
+                pltpu.SemaphoreType.DMA((2, len(links))),
+                pltpu.SemaphoreType.DMA((2, len(links))),
+            ],
+            0,
+        )
+
+    others = curve_count * strip_count - 1
+    if others < DIRECT_LIMIT and total_rows <= LANES and outer_levels * 64 == LANES:
+        change, sideways = call(
+            direct_kernel,
+            build_direct_tables(),
+            (pltpu.VMEM(nodes_first.shape, f32), jax.ShapeDtypeStruct((1,), jnp.int32)),
+            (vmem, pl.BlockSpec(memory_space=pltpu.SMEM)),
+            [
+                pltpu.VMEM((total_rows, LANES), f32),
+                pltpu.VMEM((total_rows, LANES), f32),
+                pltpu.VMEM((8, LANES), f32),
+                pltpu.VMEM((-(-others // 8) * 8, LANES), f32),
+                pltpu.VMEM((outer_levels * LANES, 4 * columns), bf16),
+                pltpu.VMEM((128, 4 * columns), f32),
+                pltpu.VMEM((32, 4 * columns), f32),
+                pltpu.SemaphoreType.DMA((5,)),
+                pltpu.SemaphoreType.DMA((len(links),)),
+                pltpu.SemaphoreType.DMA((len(links),)),
+                pltpu.SemaphoreType.DMA((others,)),
+                pltpu.SemaphoreType.DMA((others,)),
+            ],
+            1,
+        )
+        change = lax.cond(sideways[0] == 0, lambda kept: kept, lambda _: two_rounds(), change)
+    else:
+        change = two_rounds()
+    next_register = section_a * register + step_size * jnp.transpose(change, (1, 0, 2))
     return state + section_b * next_register, next_register
 
 

time: 19.1 us -> 15.3 us (0.80)
  Pallas kernels: 16.7 us -> 12.2 us
  other arithmetic: 1.63 us -> 0.76 us
  local copies, waits for them, and re-layouts: 0.01 us -> 0.87 us
  between operations: 0.67 us -> 1.29 us
    pallas_call x1, Pallas kernels: 16.7 us -> 12.2 us  [call(): pl.pallas_call(functools.partial(kernel, plan), out_shape=outputs, in_spe...]
    add x1, other arithmetic: 1.63 us -> 0.76 us  [body(): return (state + section_b * next_register, next_register)]
    unnamed x4, local copies, waits for them, and re-layouts: 0.01 us -> 0.87 us
where the time goes in v2:
time: 15.3 us; the launch traced here: 15.1 us
  Pallas kernels  12.2 us (80%)
  between operations  1.29 us (8%)
  local copies, waits for them, and re-layouts  0.87 us (6%)
  other arithmetic  0.76 us (5%)
    pallas_call x1, Pallas kernels, call(): pl.pallas_call(functools.partial(kernel, plan), out_shape=outputs, in_spe...  12.2 us
    unnamed x4, local copies, waits for them, and re-layouts  0.87 us
    add x1, other arithmetic, body(): return (state + section_b * next_register, next_register)  0.76 us

profile of v2, /device:TPU:0, one launch (start us, length us, event | category | flops | bytes accessed | tf_op | source)
XLA Modules:
  0.0 15.1 jit_solution(11406430209491408380)
XLA Ops:
  0.6 0.0 copy-start
  0.6 12.2 %shard_map.88 = (f32[25,4,256]{2,1,0:T(4,128)S(1)}, s32[1]{0:T(128)}) custom-call(f32[25,4,256]{2,1,0:T(4,128)} %bitcast.5, s32[4,64]{1,0:T(4,128)} %neighbor_hbm.1, s32[4,64]{1,0:T(4,128)} %neighbor_face_hbm.1, s32[4,64]{1,0:T(4,128)} %seam_hbm.1, bf16[128,384]{1,0:T(8,128)(2,1)} %constant.13.clone.tables_hbm), custom_call_target="tpu_custom_call" | custom-call | tf_op jit(solution)/shard_map/pallas_call | solution.py:876
  13.4 0.0 copy-done
  13.4 0.0 copy-start.1
  13.5 0.9 %copy-done.1 = f32[4,25,256]{2,0,1:T(4,128)S(1)} copy-done((f32[4,25,256]{2,0,1:T(4,128)S(1)}, f32[4,25,256]{2,0,1:T(4,128)}, u32[]{:S(2)}) %copy-start.1) | copy-done | bytes 102424
  14.3 0.8 %multiply_add_fusion = (f32[4,25,256]{2,0,1:T(4,128)}, f32[4,25,256]{2,0,1:T(4,128)}) fusion(f32[4,25,256]{2,0,1:T(4,128)S(1)} %copy-done, f32[25,4,256]{2,1,0:T(4,128)S(1)} %get-tuple-element.37, f32[4,25,256]{2,0,1:T(4,128)S(1)} %copy-done.1), kind=kLoop, calls=%fused_computation.1 | loop fusion | flops 128000 | bytes 512000 | tf_op jit(solution)/shard_map/add | solution.py:941
  (1 shorter events, 0.0 us)
Async XLA Ops:
  0.6 12.8 %copy-start = (f32[4,25,256]{2,0,1:T(4,128)S(1)}, f32[4,25,256]{2,0,1:T(4,128)}, u32[]{:S(2)}) copy-start(f32[4,25,256]{2,0,1:T(4,128)} %param.9) | copy-start | bytes 307204
  13.4 0.9 %copy-start.1 = (f32[4,25,256]{2,0,1:T(4,128)S(1)}, f32[4,25,256]{2,0,1:T(4,128)}, u32[]{:S(2)}) copy-start(f32[4,25,256]{2,0,1:T(4,128)} %param.10) | copy-start | bytes 307204

commit v3 on v2

--- a/solution.py
+++ b/solution.py
@@ -492,7 +492,9 @@
     neighbor_face_hbm,
     seam_hbm,
     tables_hbm,
-    change,
+    register_hbm,
+    own_part,
+    late_part,
     sideways,
     state,
     neighbor,
@@ -506,7 +508,7 @@
     notices,
     spread,
     known,
-    base_change,
+    register,
     load_sem,
     send_sem,
     recv_sem,
@@ -555,6 +557,7 @@
                 (seam_hbm, seam),
                 (state_hbm, state),
                 (tables_hbm, tables),
+                (register_hbm, register),
             ]
         )
     ]
@@ -701,7 +704,7 @@
             axis=0,
         )
 
-    for load in loads[3:]:
+    for load in loads[3:5]:
         load.wait()
     for field in range(4):
         padded[field, :25] = state[:, field, :]
@@ -791,9 +794,14 @@
         nothing = jnp.zeros_like(pressure)
         flux_x = jnp.concatenate([vel_u, pressure, nothing, theta * vel_u], axis=1)
         flux_y = jnp.concatenate([vel_v, nothing, pressure, theta * vel_v], axis=1)
-        base_change[...] = dot3(
-            tables[64:96, :288], jnp.concatenate([flux_x, flux_y, values], axis=0)
-        )
+        loads[5].wait()
+        for field in range(4):
+            padded[field, :25] = register[:, field, :]
+        held = jnp.concatenate([padded[field] for field in range(4)], axis=1)
+        own = dot3(tables[64:96, :288], jnp.concatenate([flux_x, flux_y, values], axis=0))
+        own = section_a * held + step_size * own
+        for field in range(4):
+            own_part[:, field, :] = own[:25, field * columns : (field + 1) * columns]
 
     for index in range(link_count):
         copy_of(index).wait_recv()
@@ -833,11 +841,11 @@
             rows.append(term if drops[field] is None else term + drops[field])
         terms.append(jnp.concatenate(rows, axis=0))
     face_term = jnp.concatenate(terms, axis=1)
-    total = base_change[...] + dot3(
+    late = dot3(
         tables[96:128, :192], jnp.concatenate([to_faces(face_term), to_faces(jump)], axis=0)
     )
     for field in range(4):
-        change[:, field, :] = total[:25, field * columns : (field + 1) * columns]
+        late_part[:, field, :] = late[:25, field * columns : (field + 1) * columns]
 
     for index in range(len(others)):
         notice_of(index).wait_recv()
@@ -870,13 +878,15 @@
     plan = (elems, levels, curve_count, strip_count, links, rows_of, offsets)
     vmem = pl.BlockSpec(memory_space=pltpu.VMEM)
     nodes_first = jnp.transpose(state, (1, 0, 2))
-
-    def call(kernel, tables, outputs, out_specs, scratch, collective_id):
-        operands = (nodes_first, neighbor, neighbor_face, seam, jnp.asarray(tables))
+    register_first = jnp.transpose(register, (1, 0, 2))
+    shape = nodes_first.shape
+
+    def call(kernel, tables, more, outputs, out_specs, scratch, collective_id):
+        operands = (nodes_first, neighbor, neighbor_face, seam, jnp.asarray(tables), *more)
         return pl.pallas_call(
             functools.partial(kernel, plan),
             out_shape=outputs,
-            in_specs=[pl.BlockSpec(memory_space=pl.ANY)] * 5,
+            in_specs=[pl.BlockSpec(memory_space=pl.ANY)] * len(operands),
             out_specs=out_specs,
             scratch_shapes=[
                 pltpu.VMEM(nodes_first.shape, f32),
@@ -893,9 +903,10 @@
         )(*[pltpu.with_memory_space_constraint(operand, pltpu.HBM) for operand in operands])
 
     def two_rounds():
-        return call(
+        change = call(
             two_round_kernel,
             build_tables(),
+            (),
             pltpu.VMEM(nodes_first.shape, f32),
             vmem,
             [
@@ -910,14 +921,16 @@
             ],
             0,
         )
+        return section_a * register_first, change
 
     others = curve_count * strip_count - 1
     if others < DIRECT_LIMIT and total_rows <= LANES and outer_levels * 64 == LANES:
-        change, sideways = call(
+        *parts, sideways = call(
             direct_kernel,
             build_direct_tables(),
-            (pltpu.VMEM(nodes_first.shape, f32), jax.ShapeDtypeStruct((1,), jnp.int32)),
-            (vmem, pl.BlockSpec(memory_space=pltpu.SMEM)),
+            (register_first,),
+            (pltpu.VMEM(shape, f32), pltpu.VMEM(shape, f32), pltpu.SMEM((1,), jnp.int32)),
+            (vmem, vmem, pl.BlockSpec(memory_space=pltpu.SMEM)),
             [
                 pltpu.VMEM((total_rows, LANES), f32),
                 pltpu.VMEM((total_rows, LANES), f32),
@@ -925,8 +938,8 @@
                 pltpu.VMEM((-(-others // 8) * 8, LANES), f32),
                 pltpu.VMEM((outer_levels * LANES, 4 * columns), bf16),
                 pltpu.VMEM((128, 4 * columns), f32),
-                pltpu.VMEM((32, 4 * columns), f32),
-                pltpu.SemaphoreType.DMA((5,)),
+                pltpu.VMEM(shape, f32),
+                pltpu.SemaphoreType.DMA((6,)),
                 pltpu.SemaphoreType.DMA((len(links),)),
                 pltpu.SemaphoreType.DMA((len(links),)),
                 pltpu.SemaphoreType.DMA((others,)),
@@ -934,10 +947,12 @@
             ],
             1,
         )
-        change = lax.cond(sideways[0] == 0, lambda kept: kept, lambda _: two_rounds(), change)
+        own, late = lax.cond(
+            sideways[0] == 0, lambda kept: tuple(kept), lambda _: two_rounds(), parts
+        )
     else:
-        change = two_rounds()
-    next_register = section_a * register + step_size * jnp.transpose(change, (1, 0, 2))
+        own, late = two_rounds()
+    next_register = jnp.transpose(own, (1, 0, 2)) + step_size * jnp.transpose(late, (1, 0, 2))
     return state + section_b * next_register, next_register
 
 

time: 15.3 us -> 13.2 us (0.86)
  local copies, waits for them, and re-layouts: 0.87 us -> 0.01 us
  between operations: 1.29 us -> 0.68 us
  Pallas kernels: 12.2 us -> 11.6 us
    unnamed x4, local copies, waits for them, and re-layouts: 0.87 us -> 0.01 us
    pallas_call x1, Pallas kernels: 12.2 us -> 11.6 us  [call(): pl.pallas_call(functools.partial(kernel, plan), out_shape=outputs, in_spe...]
where the time goes in v3:
time: 13.2 us; the launch traced here: 13.1 us
  Pallas kernels  11.6 us (88%)
  other arithmetic  0.75 us (6%)
  between operations  0.68 us (5%)
    pallas_call x1, Pallas kernels, call(): pl.pallas_call(functools.partial(kernel, plan), out_shape=outputs, in_spe...  11.6 us
    add x1, other arithmetic, body(): return (state + section_b * next_register, next_register)  0.75 us

profile of v3, /device:TPU:0, one launch (start us, length us, event | category | flops | bytes accessed | tf_op | source)
XLA Modules:
  0.0 13.1 jit_solution(5787568346473673597)
XLA Ops:
  0.6 0.0 copy-start
  0.6 0.0 copy-start.1
  0.6 11.6 %shard_map.88 = (f32[25,4,256]{2,1,0:T(4,128)S(1)}, f32[25,4,256]{2,1,0:T(4,128)S(1)}, s32[1]{0:T(128)S(4)}) custom-call(f32[25,4,256]{2,1,0:T(4,128)} %bitcast.6, s32[4,64]{1,0:T(4,128)} %neighbor_hbm.1, s32[4,64]{1,0:T(4,128)} %neighbor_face_hbm.1, s32[4,64]{1,0:T(4,128)} %seam_hbm.1, bf16[128,384]{1,0:T(8,128)(2,1)} %constant.13.clone.tables_hbm, ...), custom_call_target="tpu_custom_call" | custom-call | tf_op jit(solution)/shard_map/pallas_call | solution.py:886
  12.3 0.0 copy-done
  12.3 0.0 copy-done.1
  12.3 0.7 %multiply_add_fusion = (f32[4,25,256]{2,0,1:T(4,128)}, f32[4,25,256]{2,0,1:T(4,128)}) fusion(f32[4,25,256]{2,0,1:T(4,128)S(1)} %copy-done, f32[25,4,256]{2,1,0:T(4,128)S(1)} %get-tuple-element.32, f32[25,4,256]{2,1,0:T(4,128)S(1)} %get-tuple-element.33), kind=kLoop, calls=%fused_computation.1 | loop fusion | flops 102400 | bytes 512000 | tf_op jit(solution)/shard_map/add | solution.py:956
  (1 shorter events, 0.0 us)
Async XLA Ops:
  0.6 11.7 %copy-start = (f32[4,25,256]{2,0,1:T(4,128)S(1)}, f32[4,25,256]{2,0,1:T(4,128)}, u32[]{:S(2)}) copy-start(f32[4,25,256]{2,0,1:T(4,128)} %param.9) | copy-start | bytes 307204
  0.6 11.7 %copy-start.1 = (f32[4,25,256]{2,0,1:T(4,128)S(1)}, f32[4,25,256]{2,0,1:T(4,128)}, u32[]{:S(2)}) copy-start(f32[4,25,256]{2,0,1:T(4,128)} %param.10) | copy-start | bytes 307204

commit v4 on v3

--- a/solution.py
+++ b/solution.py
@@ -94,11 +94,17 @@
     base = np.concatenate([-dx, -dy, viscosity * (dx @ dx + dy @ dy)], axis=1)
     jump = viscosity * (dx @ lift_x + dy @ lift_y)
     late = np.concatenate([lift_gain * pick.T, jump], axis=1)
-    out = np.zeros((128, 384), ml_dtypes.bfloat16)
-    out[:64, :96] = split_const(np.concatenate([pick, slope], axis=0))
-    out[64:96, :288] = split_const(base)
-    out[96:128, :192] = split_const(late)
-    return out
+    mirror = np.arange(32).reshape(4, 8)
+    mirror[:, :5] = mirror[:, 4::-1]
+    mirror = mirror.reshape(-1)
+    first = np.zeros((128, LANES), ml_dtypes.bfloat16)
+    first[:, :96] = split_const(
+        np.concatenate([pick, slope, pick[mirror], slope[mirror]], axis=0)
+    )
+    out = np.zeros((64, 384), ml_dtypes.bfloat16)
+    out[:32, :288] = split_const(base)
+    out[32:, :192] = split_const(late)
+    return first, out
 
 
 def halves(x):
@@ -491,29 +497,33 @@
     neighbor_hbm,
     neighbor_face_hbm,
     seam_hbm,
+    face_tables_hbm,
     tables_hbm,
     register_hbm,
     own_part,
     late_part,
     sideways,
     state,
-    neighbor,
-    neighbor_face,
-    seam,
+    indices,
+    face_tables,
     tables,
     padded,
     sent,
     arrived,
     notice,
     notices,
+    verdict,
     spread,
     known,
     register,
+    index_sem,
     load_sem,
     send_sem,
     recv_sem,
     notice_send_sem,
     notice_recv_sem,
+    verdict_send_sem,
+    verdict_recv_sem,
 ):
     elems, levels, curve_count, strip_count, links, rows_of, offsets = plan
     columns = elems * levels
@@ -536,66 +546,118 @@
         )
 
     places = [place_at(step, 0) if axis == "curve" else place_at(0, step) for axis, step in links]
-    others = [
-        place_at(curve_step, strip_step)
-        for curve_step in range(curve_count)
-        for strip_step in range(strip_count)
-        if curve_step or strip_step
-    ]
-
-    barrier = pltpu.get_barrier_semaphore()
-    for place in others:
+    device_count = curve_count * strip_count
+    herald = device_count // 2 - 1
+    collectors = (0, 1, herald)
+    collects = (device_pos < 2) | (device_pos == herald)
+
+    def place_of(position):
+        return (position // strip_count, position % strip_count)
+
+    def tell(place):
         pl.semaphore_signal(
             barrier, inc=1, device_id=place, device_id_type=pl.DeviceIdType.MESH
         )
-    loads = [
-        pltpu.make_async_copy(source_ref, target_ref, load_sem.at[index])
-        for index, (source_ref, target_ref) in enumerate(
-            [
-                (neighbor_hbm, neighbor),
-                (neighbor_face_hbm, neighbor_face),
-                (seam_hbm, seam),
-                (state_hbm, state),
-                (tables_hbm, tables),
-                (register_hbm, register),
-            ]
-        )
-    ]
-    for load in loads:
-        load.start()
-    padded[...] = jnp.zeros_like(padded)
+
+    def notice_to(position):
+        return pltpu.make_async_remote_copy(
+            src_ref=notice.at[pl.ds(0, 1)],
+            dst_ref=notices.at[pl.ds(device_pos, 1)],
+            send_sem=notice_send_sem,
+            recv_sem=notice_recv_sem,
+            device_id=place_of(position),
+            device_id_type=pl.DeviceIdType.MESH,
+        )
+
+    def verdict_to(position):
+        return pltpu.make_async_remote_copy(
+            src_ref=notice.at[pl.ds(8, 1)],
+            dst_ref=verdict.at[pl.ds(0, 1)],
+            send_sem=verdict_send_sem,
+            recv_sem=verdict_recv_sem,
+            device_id=place_of(position),
+            device_id_type=pl.DeviceIdType.MESH,
+        )
+
+    def rows_done(ref, count, semaphore):
+        rows = ref.at[pl.ds(0, count)]
+        return pltpu.make_async_copy(rows, rows, semaphore)
 
     def copy_of(index):
         rows = pl.ds(offsets[index], rows_of[index])
         return pltpu.make_async_remote_copy(
             src_ref=sent.at[rows],
             dst_ref=arrived.at[rows],
-            send_sem=send_sem.at[index],
-            recv_sem=recv_sem.at[index],
+            send_sem=send_sem,
+            recv_sem=recv_sem,
             device_id=places[index],
             device_id_type=pl.DeviceIdType.MESH,
         )
 
-    def notice_of(index):
-        return pltpu.make_async_remote_copy(
-            src_ref=notice.at[pl.ds(0, 1)],
-            dst_ref=notices.at[pl.ds(index, 1)],
-            send_sem=notice_send_sem.at[index],
-            recv_sem=notice_recv_sem.at[index],
-            device_id=others[index],
-            device_id_type=pl.DeviceIdType.MESH,
-        )
-
-    for load in loads[:3]:
-        load.wait()
-
-    def widen(ref):
-        block = ref[...]
-        return jnp.concatenate([block] * inner, axis=1)
-
-    across = widen(neighbor)
-    face_back = widen(neighbor_face)
-    codes = widen(seam)
+    index_loads = [
+        pltpu.make_async_copy(source_ref, indices.at[index], index_sem)
+        for index, source_ref in enumerate((neighbor_hbm, neighbor_face_hbm, seam_hbm))
+    ]
+    loads = [
+        pltpu.make_async_copy(source_ref, target_ref, load_sem.at[index])
+        for index, (source_ref, target_ref) in enumerate(
+            [
+                (face_tables_hbm, face_tables),
+                (tables_hbm, tables),
+                (register_hbm, register),
+            ]
+        )
+    ]
+    nodes = state.shape[0]
+    piece = -(-nodes // 5)
+    state_loads = [
+        pltpu.make_async_copy(
+            state_hbm.at[pl.ds(start, min(piece, nodes - start))],
+            state.at[pl.ds(start, min(piece, nodes - start))],
+            load_sem.at[3],
+        )
+        for start in range(0, nodes, piece)
+    ]
+    for load in index_loads + state_loads + loads:
+        load.start()
+    notices[...] = jnp.zeros_like(notices)
+    barrier = pltpu.get_barrier_semaphore()
+    for place in places:
+        tell(place)
+    for collector in collectors:
+
+        @pl.when(device_pos == collector)
+        def _():
+            for position in range(device_count - 1, -1, -1):
+                if position != collector:
+                    tell(place_of(position))
+
+    padded[...] = jnp.zeros_like(padded)
+    level = iota((8, columns), 1) % levels
+    link_iota = iota((link_rows, LANES), 0)
+    wide_iota = iota((link_rows, columns), 0)
+    target = jnp.full((link_rows, LANES), -1, jnp.int32)
+    base_wide = jnp.zeros((link_rows, columns), f32)
+    base_back = jnp.zeros((link_rows, LANES), f32)
+    for index, place in enumerate(places):
+        target = jnp.where(link_iota == index, place[0] * strip_count + place[1], target)
+        base_wide = jnp.where(wide_iota == index, float(offsets[index] + 1), base_wide)
+        base_back = jnp.where(link_iota == index, float(offsets[index ^ 1] + 1), base_back)
+    from_elem = iota((LANES, columns), 0)
+    to_elem = iota((LANES, columns), 1) // levels
+    reach = jnp.concatenate(
+        [
+            onehot((from_elem < elems) & (from_elem < to_elem)),
+            onehot(from_elem < elems),
+            onehot(from_elem == to_elem),
+        ],
+        axis=1,
+    )
+    pltpu.make_async_copy(indices, indices, index_sem).wait()
+
+    across, face_back, codes = [
+        jnp.concatenate([indices[index]] * inner, axis=1) for index in range(3)
+    ]
     owner = across // elems
     place_in = across % elems
     turn = codes % 4
@@ -603,55 +665,54 @@
     own_face = iota((4, LANES), 0)
     quarter = (face_back + turn - own_face + 4) % 4
     odd = jnp.where(quarter % 2 == 1, 1.0, 0.0)
-    notice[...] = jnp.broadcast_to(jnp.sum(odd, axis=0, keepdims=True), (8, LANES))
+    notice[:8] = jnp.broadcast_to(jnp.sum(odd, axis=0, keepdims=True), (8, LANES))
+    early = device_pos >= device_count - strip_count // 2
+
+    def meet_and_notify():
+        pl.semaphore_wait(barrier, link_count + len(collectors) - jnp.where(collects, 1, 0))
+        for collector in collectors:
+
+            @pl.when(device_pos != collector)
+            def _():
+                notice_to(collector).start()
+
+    pl.when(early)(meet_and_notify)
     side = jnp.where(quarter == 0, 1.0, -1.0)
     cosine = jnp.where(turn == 0, 1.0, 0.0) - jnp.where(turn == 2, 1.0, 0.0)
     sine = jnp.where(turn == 3, 1.0, 0.0) - jnp.where(turn == 1, 1.0, 0.0)
 
-    link_iota = iota((link_rows, LANES), 0)
-    target = jnp.full((link_rows, LANES), -1, jnp.int32)
-    base = jnp.zeros((link_rows, LANES), f32)
-    base_back = jnp.zeros((link_rows, LANES), f32)
-    for index, place in enumerate(places):
-        here = link_iota == index
-        target = jnp.where(here, place[0] * strip_count + place[1], target)
-        base = jnp.where(here, float(offsets[index] + 1), base)
-        base_back = jnp.where(here, float(offsets[index ^ 1] + 1), base_back)
     member = [
         jnp.where(owner[face : face + 1] == target, 1.0, 0.0) for face in range(4)
     ]
-    from_lane = iota((LANES, 2 * LANES), 0)
-    to_lane = iota((LANES, 2 * LANES), 1)
-    same = from_lane // elems == (to_lane % LANES) // elems
-    earlier = same & ((from_lane < to_lane) | (to_lane >= LANES))
-    counts = dot(jnp.concatenate(member, axis=0).astype(bf16), onehot(earlier))
-    before = jnp.zeros((link_rows, LANES), f32)
-    slot_rows = []
+    extras = [
+        jnp.concatenate([part, jnp.zeros_like(part)], axis=0)
+        for part in (flipped.astype(f32), cosine, sine, side)
+    ]
+    wide = dot(jnp.concatenate(member + extras, axis=0).astype(bf16), reach)
+    before = jnp.zeros((link_rows, columns), f32)
+    spots = []
     for face in range(4):
-        part = counts[face * link_rows : (face + 1) * link_rows]
-        rank = part[:, :LANES] + before
-        before = before + part[:, LANES:]
-        slot_rows.append(
-            jnp.sum(member[face] * (base + inner * rank), axis=0, keepdims=True)
-        )
-
-    stretch = onehot(iota((LANES, columns), 0) == iota((LANES, columns), 1) // levels)
+        part = wide[face * link_rows : (face + 1) * link_rows]
+        rank = part[:, :columns] + before
+        before = before + part[:, columns : 2 * columns]
+        chosen = part[:, 2 * columns :] * (base_wide + inner * rank)
+        spots.append(jnp.sum(chosen, axis=0, keepdims=True))
+    extra_row = 4 * link_rows
+    flip_wide, cos_wide, sin_wide, side_wide = [
+        wide[extra_row + 8 * index : extra_row + 8 * index + 8, 2 * columns :]
+        for index in range(4)
+    ]
 
     def stretched(per_face):
         rows = []
         for values in per_face:
             rows.append(values)
             rows.append(jnp.zeros_like(values))
-        wide = dot(jnp.concatenate(rows, axis=0).astype(bf16), stretch)
+        wide = dot(jnp.concatenate(rows, axis=0).astype(bf16), reach[:, 2 * columns :])
         return [wide[8 * index : 8 * index + 8] for index in range(len(per_face))]
 
-    slot, flip_wide, cos_wide, sin_wide, side_wide = stretched(
-        [jnp.concatenate(slot_rows, axis=0), flipped.astype(f32), cosine, sine, side]
-    )
-    level = iota((8, columns), 1) % levels
-
     def rows_for(slot, stride):
-        spot = slot + (level % inner + level // inner * stride).astype(f32)
+        spot = slot + (level[:1] % inner + level[:1] // inner * stride).astype(f32)
         return jnp.where(slot > 0.5, spot, 0.0)
 
     def hot_rows(count, spots):
@@ -659,14 +720,14 @@
         return jnp.concatenate(
             [
                 onehot(
-                    count_iota == jnp.broadcast_to(spots[face : face + 1], (count, columns))
+                    count_iota == jnp.broadcast_to(spots[face], (count, columns))
                 )
                 for face in range(4)
             ],
             axis=1,
         )
 
-    pack = hot_rows(outer_levels * total_rows, rows_for(slot, total_rows))
+    pack = hot_rows(total_rows, [rows_for(spot, 0) for spot in spots])
 
     def over_faces(wide, rows):
         return jnp.concatenate(
@@ -704,46 +765,49 @@
             axis=0,
         )
 
-    for load in loads[3:5]:
-        load.wait()
+    flip_all, cos_all, sin_all, side_all = [
+        over_faces(wide, 8) for wide in (flip_wide, cos_wide, sin_wide, side_wide)
+    ]
+    level_all = iota((half, span), 1) % levels // inner
+
+    loads[0].wait()
+    pltpu.make_async_copy(state, state, load_sem.at[3]).wait()
     for field in range(4):
         padded[field, :25] = state[:, field, :]
     values = jnp.concatenate([padded[field] for field in range(4)], axis=1)
-    on_faces = dot3(tables[:64, :96], values)
-    traces = to_fields(on_faces[:32])
-    slopes = to_fields(on_faces[32:])
-    row32 = iota((32, span), 0)
-    marked = jnp.where(row32 == 5, over_faces(flip_wide, 32), traces)
-    marked = jnp.where(row32 == 13, over_faces(cos_wide, 32), marked)
-    marked = jnp.where(row32 == 21, over_faces(sin_wide, 32), marked)
-    slopes_out = slopes * over_faces(side_wide, 32)
-    high, low = halves(jnp.concatenate([marked, slopes_out], axis=0))
-    stacked = dot_t(pack, jnp.concatenate([high, low], axis=0))
-    lane = iota((total_rows, LANES), 1)
-    message = jnp.zeros((total_rows, LANES), f32)
-    for index in range(outer_levels):
-        part = stacked[index * total_rows : (index + 1) * total_rows]
-        part = part + pltpu.roll(part, half, axis=1)
-        message = jnp.where(lane // half == index, part, message)
-    flip, cos, sin = [
-        jnp.broadcast_to(message[:, spot : spot + 1], message.shape) for spot in (5, 13, 21)
-    ]
-    node_lane = lane % 8
-    field_lane = lane % 32 // 8
-    mirrored = message
-    for node, shift in ((0, LANES - 4), (1, LANES - 2), (3, 2), (4, 4)):
-        mirrored = jnp.where(node_lane == node, pltpu.roll(message, shift, axis=1), mirrored)
-    aligned = jnp.where(flip > 0.5, mirrored, message)
-    turned_u = cos * aligned - sin * pltpu.roll(aligned, LANES - 8, axis=1)
-    turned_v = cos * aligned + sin * pltpu.roll(aligned, 8, axis=1)
-    sent[...] = jnp.where(
-        field_lane == 1, turned_u, jnp.where(field_lane == 2, turned_v, aligned)
-    )
-    pl.semaphore_wait(barrier, len(others))
+    on_faces = dot3(face_tables[:, :96], values)
+    traces, slopes, flipped_traces, flipped_slopes = [
+        to_fields(on_faces[32 * part : 32 * part + 32]) for part in range(4)
+    ]
+
+    def aligned(plain, mirrored):
+        parts = [
+            jnp.where(
+                flip_all > 0.5,
+                mirrored[field * 8 : field * 8 + 8],
+                plain[field * 8 : field * 8 + 8],
+            )
+            for field in range(4)
+        ]
+        parts[1], parts[2] = (
+            cos_all * parts[1] - sin_all * parts[2],
+            cos_all * parts[2] + sin_all * parts[1],
+        )
+        return parts
+
+    message = aligned(traces, flipped_traces) + [
+        side_all * part for part in aligned(slopes, flipped_slopes)
+    ]
+    high, low = halves(jnp.concatenate(message, axis=0))
+    pieces = []
+    for part in (high, low):
+        for index in range(outer_levels):
+            pieces.append(jnp.where(level_all == index, part, jnp.zeros_like(part)))
+    stacked = dot_t(pack, jnp.concatenate(pieces, axis=0))
+    sent[...] = stacked[:, :LANES] + stacked[:, LANES:]
+    pl.when(jnp.logical_not(early))(meet_and_notify)
     for index in range(link_count):
         copy_of(index).start()
-    for index in range(len(others)):
-        notice_of(index).start()
     always = device_pos >= 0
 
     @pl.when(always)
@@ -769,17 +833,22 @@
             for face in range(4)
         ]
         back, *homes = stretched([jnp.concatenate(back_rows, axis=0)] + homes)
-        spread[...] = hot_rows(outer_levels * LANES, rows_for(back, LANES))
-
+        spread[...] = hot_rows(
+            outer_levels * LANES,
+            [rows_for(back[face : face + 1], LANES) for face in range(4)],
+        )
+
+        slopes_out = slopes * over_faces(side_wide, 32)
         both_high, both_low = halves(jnp.concatenate([traces, slopes_out], axis=0))
         both = jnp.concatenate([both_high, both_low], axis=0)
         found = jnp.zeros((128, span), f32)
         for face in range(4):
-            spots = jnp.where(
+            home_spot = jnp.where(
                 homes[face] > 0.5, homes[face] * levels + (level - levels + 1).astype(f32), 0.0
             )
             found = found + dot(
-                both[:, face * columns : (face + 1) * columns], hot_rows(columns, spots)
+                both[:, face * columns : (face + 1) * columns],
+                hot_rows(columns, [home_spot[into : into + 1] for into in range(4)]),
             )
         found = found[:64] + found[64:]
         known[:32] = traces
@@ -794,17 +863,17 @@
         nothing = jnp.zeros_like(pressure)
         flux_x = jnp.concatenate([vel_u, pressure, nothing, theta * vel_u], axis=1)
         flux_y = jnp.concatenate([vel_v, nothing, pressure, theta * vel_v], axis=1)
-        loads[5].wait()
+        loads[1].wait()
+        loads[2].wait()
         for field in range(4):
             padded[field, :25] = register[:, field, :]
         held = jnp.concatenate([padded[field] for field in range(4)], axis=1)
-        own = dot3(tables[64:96, :288], jnp.concatenate([flux_x, flux_y, values], axis=0))
+        own = dot3(tables[:32, :288], jnp.concatenate([flux_x, flux_y, values], axis=0))
         own = section_a * held + step_size * own
         for field in range(4):
             own_part[:, field, :] = own[:25, field * columns : (field + 1) * columns]
 
-    for index in range(link_count):
-        copy_of(index).wait_recv()
+    rows_done(arrived, total_rows, recv_sem).wait()
     filler = jnp.zeros((LANES - total_rows, LANES), f32)
     turned = jnp.transpose(jnp.concatenate([arrived[...], filler], axis=0))
     turned = jnp.concatenate(
@@ -842,19 +911,38 @@
         terms.append(jnp.concatenate(rows, axis=0))
     face_term = jnp.concatenate(terms, axis=1)
     late = dot3(
-        tables[96:128, :192], jnp.concatenate([to_faces(face_term), to_faces(jump)], axis=0)
+        tables[32:, :192], jnp.concatenate([to_faces(face_term), to_faces(jump)], axis=0)
     )
     for field in range(4):
         late_part[:, field, :] = late[:25, field * columns : (field + 1) * columns]
 
-    for index in range(len(others)):
-        notice_of(index).wait_recv()
-    heard = jnp.max(notices[: len(others)]) + jnp.max(notice[...])
-    sideways[0] = jnp.where(heard > 0.5, 1, 0)
-    for index in range(link_count):
-        copy_of(index).wait_send()
-    for index in range(len(others)):
-        notice_of(index).wait_send()
+    @pl.when(collects)
+    def _():
+        rows_done(notices, device_count - 1, notice_recv_sem).wait()
+        heard = jnp.max(notices[...], axis=0, keepdims=True) + notice[:1]
+        notice[8:] = jnp.broadcast_to(heard, (8, LANES))
+
+        @pl.when(device_pos == herald)
+        def _():
+            for position in range(device_count):
+                if position not in collectors:
+                    verdict_to(position).start()
+
+        sideways[0] = jnp.where(jnp.max(heard) > 0.5, 1, 0)
+
+        @pl.when(device_pos == herald)
+        def _():
+            rows_done(notices, device_count - len(collectors), verdict_send_sem).wait()
+
+        rows_done(notice, len(collectors) - 1, notice_send_sem).wait()
+
+    @pl.when(jnp.logical_not(collects))
+    def _():
+        rows_done(notice, len(collectors), notice_send_sem).wait()
+        rows_done(verdict, 1, verdict_recv_sem).wait()
+        sideways[0] = jnp.where(jnp.max(verdict[:1]) > 0.5, 1, 0)
+
+    rows_done(sent, total_rows, send_sem).wait()
 
 
 def body(curve_count, strip_count, state, register, neighbor, neighbor_face, seam):
@@ -882,21 +970,14 @@
     shape = nodes_first.shape
 
     def call(kernel, tables, more, outputs, out_specs, scratch, collective_id):
-        operands = (nodes_first, neighbor, neighbor_face, seam, jnp.asarray(tables), *more)
+        tables = [jnp.asarray(table) for table in tables]
+        operands = (nodes_first, neighbor, neighbor_face, seam, *tables, *more)
         return pl.pallas_call(
             functools.partial(kernel, plan),
             out_shape=outputs,
             in_specs=[pl.BlockSpec(memory_space=pl.ANY)] * len(operands),
             out_specs=out_specs,
-            scratch_shapes=[
-                pltpu.VMEM(nodes_first.shape, f32),
-                pltpu.VMEM(neighbor.shape, jnp.int32),
-                pltpu.VMEM(neighbor.shape, jnp.int32),
-                pltpu.VMEM(neighbor.shape, jnp.int32),
-                pltpu.VMEM(tables.shape, bf16),
-                pltpu.VMEM((4, 32, columns), f32),
-            ]
-            + scratch,
+            scratch_shapes=scratch,
             compiler_params=pltpu.CompilerParams(
                 collective_id=collective_id, has_side_effects=True
             ),
@@ -905,11 +986,17 @@
     def two_rounds():
         change = call(
             two_round_kernel,
-            build_tables(),
+            (build_tables(),),
             (),
             pltpu.VMEM(nodes_first.shape, f32),
             vmem,
             [
+                pltpu.VMEM(shape, f32),
+                pltpu.VMEM(neighbor.shape, jnp.int32),
+                pltpu.VMEM(neighbor.shape, jnp.int32),
+                pltpu.VMEM(neighbor.shape, jnp.int32),
+                pltpu.VMEM((224, 384), bf16),
+                pltpu.VMEM((4, 32, columns), f32),
                 pltpu.VMEM((2, total_rows, LANES), f32),
                 pltpu.VMEM((2, total_rows, LANES), f32),
                 pltpu.VMEM((32, 4 * columns), f32),
@@ -923,8 +1010,8 @@
         )
         return section_a * register_first, change
 
-    others = curve_count * strip_count - 1
-    if others < DIRECT_LIMIT and total_rows <= LANES and outer_levels * 64 == LANES:
+    device_count = curve_count * strip_count
+    if device_count <= DIRECT_LIMIT and total_rows <= LANES and outer_levels * 64 == LANES:
         *parts, sideways = call(
             direct_kernel,
             build_direct_tables(),
@@ -932,18 +1019,27 @@
             (pltpu.VMEM(shape, f32), pltpu.VMEM(shape, f32), pltpu.SMEM((1,), jnp.int32)),
             (vmem, vmem, pl.BlockSpec(memory_space=pltpu.SMEM)),
             [
+                pltpu.VMEM(shape, f32),
+                pltpu.VMEM((3, *neighbor.shape), jnp.int32),
+                pltpu.VMEM((128, LANES), bf16),
+                pltpu.VMEM((64, 384), bf16),
+                pltpu.VMEM((4, 32, columns), f32),
                 pltpu.VMEM((total_rows, LANES), f32),
                 pltpu.VMEM((total_rows, LANES), f32),
+                pltpu.VMEM((16, LANES), f32),
+                pltpu.VMEM((-(-device_count // 8) * 8, LANES), f32),
                 pltpu.VMEM((8, LANES), f32),
-                pltpu.VMEM((-(-others // 8) * 8, LANES), f32),
                 pltpu.VMEM((outer_levels * LANES, 4 * columns), bf16),
                 pltpu.VMEM((128, 4 * columns), f32),
                 pltpu.VMEM(shape, f32),
-                pltpu.SemaphoreType.DMA((6,)),
-                pltpu.SemaphoreType.DMA((len(links),)),
-                pltpu.SemaphoreType.DMA((len(links),)),
-                pltpu.SemaphoreType.DMA((others,)),
-                pltpu.SemaphoreType.DMA((others,)),
+                pltpu.SemaphoreType.DMA,
+                pltpu.SemaphoreType.DMA((4,)),
+                pltpu.SemaphoreType.DMA,
+                pltpu.SemaphoreType.DMA,
+                pltpu.SemaphoreType.DMA,
+                pltpu.SemaphoreType.DMA,
+                pltpu.SemaphoreType.DMA,
+                pltpu.SemaphoreType.DMA,
             ],
             1,
         )

time: 13.2 us -> 11.8 us (0.89)
  Pallas kernels: 11.6 us -> 10.2 us
    pallas_call x1, Pallas kernels: 11.6 us -> 10.2 us  [call(): pl.pallas_call(functools.partial(kernel, plan), out_shape=outputs, in_spe...]
where the time goes in v4:
time: 11.8 us; the launch traced here: 11.7 us
  Pallas kernels  10.2 us (86%)
  other arithmetic  0.75 us (6%)
  between operations  0.68 us (6%)
    pallas_call x1, Pallas kernels, call(): pl.pallas_call(functools.partial(kernel, plan), out_shape=outputs, in_spe...  10.2 us
    add x1, other arithmetic, body(): return (state + section_b * next_register, next_register)  0.75 us

profile of v4, /device:TPU:0, one launch (start us, length us, event | category | flops | bytes accessed | tf_op | source)
XLA Modules:
  0.0 11.7 jit_solution(5798222624076101293)
XLA Ops:
  0.6 0.0 copy-start
  0.6 0.0 copy-start.1
  0.6 10.2 %shard_map.97 = (f32[25,4,256]{2,1,0:T(4,128)S(1)}, f32[25,4,256]{2,1,0:T(4,128)S(1)}, s32[1]{0:T(128)S(4)}) custom-call(f32[25,4,256]{2,1,0:T(4,128)} %bitcast.6, s32[4,64]{1,0:T(4,128)} %neighbor_hbm.1, s32[4,64]{1,0:T(4,128)} %neighbor_face_hbm.1, s32[4,64]{1,0:T(4,128)} %seam_hbm.1, bf16[128,128]{1,0:T(8,128)(2,1)} %constant.15.clone.face_tables_hbm, ...), custom_call_target="tpu_custom_call" | custom-call | tf_op jit(solution)/shard_map/pallas_call | solution.py:975
  10.9 0.0 copy-done
  10.9 0.0 copy-done.1
  10.9 0.7 %multiply_add_fusion = (f32[4,25,256]{2,0,1:T(4,128)}, f32[4,25,256]{2,0,1:T(4,128)}) fusion(f32[4,25,256]{2,0,1:T(4,128)S(1)} %copy-done, f32[25,4,256]{2,1,0:T(4,128)S(1)} %get-tuple-element.32, f32[25,4,256]{2,1,0:T(4,128)S(1)} %get-tuple-element.33), kind=kLoop, calls=%fused_computation.1 | loop fusion | flops 102400 | bytes 512000 | tf_op jit(solution)/shard_map/add | solution.py:1052
  (1 shorter events, 0.0 us)
Async XLA Ops:
  0.6 10.3 %copy-start = (f32[4,25,256]{2,0,1:T(4,128)S(1)}, f32[4,25,256]{2,0,1:T(4,128)}, u32[]{:S(2)}) copy-start(f32[4,25,256]{2,0,1:T(4,128)} %param.10) | copy-start | bytes 307204
  0.6 10.3 %copy-start.1 = (f32[4,25,256]{2,0,1:T(4,128)S(1)}, f32[4,25,256]{2,0,1:T(4,128)}, u32[]{:S(2)}) copy-start(f32[4,25,256]{2,0,1:T(4,128)} %param.11) | copy-start | bytes 307204

commit v5 on v4

--- a/solution.py
+++ b/solution.py
@@ -516,6 +516,7 @@
     spread,
     known,
     register,
+    ready,
     index_sem,
     load_sem,
     send_sem,
@@ -554,6 +555,18 @@
     def place_of(position):
         return (position // strip_count, position % strip_count)
 
+    def beyond(index):
+        axis, step = links[index]
+        if axis == "curve" and step > 0:
+            return curve_pos + step >= curve_count
+        return None
+
+    def before_start(index):
+        axis, step = links[index]
+        if axis == "curve" and step < 0:
+            return curve_pos + step < 0
+        return None
+
     def tell(place):
         pl.semaphore_signal(
             barrier, inc=1, device_id=place, device_id_type=pl.DeviceIdType.MESH
@@ -596,7 +609,7 @@
 
     index_loads = [
         pltpu.make_async_copy(source_ref, indices.at[index], index_sem)
-        for index, source_ref in enumerate((neighbor_hbm, neighbor_face_hbm, seam_hbm))
+        for index, source_ref in enumerate((neighbor_face_hbm, seam_hbm, neighbor_hbm))
     ]
     loads = [
         pltpu.make_async_copy(source_ref, target_ref, load_sem.at[index])
@@ -622,8 +635,11 @@
         load.start()
     notices[...] = jnp.zeros_like(notices)
     barrier = pltpu.get_barrier_semaphore()
-    for place in places:
-        tell(place)
+    for index, place in enumerate(places):
+        if beyond(index) is None:
+            tell(place)
+        else:
+            pl.when(jnp.logical_not(beyond(index)))(functools.partial(tell, place))
     for collector in collectors:
 
         @pl.when(device_pos == collector)
@@ -655,7 +671,7 @@
     )
     pltpu.make_async_copy(indices, indices, index_sem).wait()
 
-    across, face_back, codes = [
+    face_back, codes, across = [
         jnp.concatenate([indices[index]] * inner, axis=1) for index in range(3)
     ]
     owner = across // elems
@@ -668,19 +684,42 @@
     notice[:8] = jnp.broadcast_to(jnp.sum(odd, axis=0, keepdims=True), (8, LANES))
     early = device_pos >= device_count - strip_count // 2
 
-    def meet_and_notify():
-        pl.semaphore_wait(barrier, link_count + len(collectors) - jnp.where(collects, 1, 0))
+    def meet():
+        count = link_count + len(collectors) - jnp.where(collects, 1, 0)
+        for index in range(link_count):
+            if before_start(index) is not None:
+                count = count - jnp.where(before_start(index), 1, 0)
+        pl.semaphore_wait(barrier, count)
+        for index in range(link_count):
+            if beyond(index) is not None:
+
+                @pl.when(beyond(index))
+                def _():
+                    pl.semaphore_signal(
+                        ready.at[links[index][1] - 1],
+                        inc=1,
+                        device_id=places[index],
+                        device_id_type=pl.DeviceIdType.MESH,
+                    )
+
+    def notify():
         for collector in collectors:
 
             @pl.when(device_pos != collector)
             def _():
                 notice_to(collector).start()
 
-    pl.when(early)(meet_and_notify)
+    @pl.when(early)
+    def _():
+        meet()
+        notify()
+
     side = jnp.where(quarter == 0, 1.0, -1.0)
     cosine = jnp.where(turn == 0, 1.0, 0.0) - jnp.where(turn == 2, 1.0, 0.0)
     sine = jnp.where(turn == 3, 1.0, 0.0) - jnp.where(turn == 1, 1.0, 0.0)
 
+    loads[0].wait()
+    pltpu.make_async_copy(state, state, load_sem.at[3]).wait()
     member = [
         jnp.where(owner[face : face + 1] == target, 1.0, 0.0) for face in range(4)
     ]
@@ -770,8 +809,6 @@
     ]
     level_all = iota((half, span), 1) % levels // inner
 
-    loads[0].wait()
-    pltpu.make_async_copy(state, state, load_sem.at[3]).wait()
     for field in range(4):
         padded[field, :25] = state[:, field, :]
     values = jnp.concatenate([padded[field] for field in range(4)], axis=1)
@@ -805,9 +842,16 @@
             pieces.append(jnp.where(level_all == index, part, jnp.zeros_like(part)))
     stacked = dot_t(pack, jnp.concatenate(pieces, axis=0))
     sent[...] = stacked[:, :LANES] + stacked[:, LANES:]
-    pl.when(jnp.logical_not(early))(meet_and_notify)
-    for index in range(link_count):
-        copy_of(index).start()
+    pl.when(jnp.logical_not(early))(meet)
+    order = sorted(
+        range(link_count), key=lambda index: (links[index][1] < 0, abs(links[index][1]))
+    )
+    for index in order:
+        if before_start(index) is None:
+            copy_of(index).start()
+        else:
+            pl.when(jnp.logical_not(before_start(index)))(copy_of(index).start)
+    pl.when(jnp.logical_not(early))(notify)
     always = device_pos >= 0
 
     @pl.when(always)
@@ -872,6 +916,14 @@
         own = section_a * held + step_size * own
         for field in range(4):
             own_part[:, field, :] = own[:25, field * columns : (field + 1) * columns]
+
+    for index in order:
+        if before_start(index) is not None:
+
+            @pl.when(before_start(index))
+            def _():
+                pl.semaphore_wait(ready.at[-links[index][1] - 1], 1)
+                copy_of(index).start()
 
     rows_done(arrived, total_rows, recv_sem).wait()
     filler = jnp.zeros((LANES - total_rows, LANES), f32)
@@ -945,6 +997,20 @@
     rows_done(sent, total_rows, send_sem).wait()
 
 
+def closing_kernel(own, late, state, next_state, next_register, new_state, new_register, sems):
+    nodes = own.shape[0]
+    piece = -(-nodes // 3)
+    for start in range(0, nodes, piece):
+        rows = pl.ds(start, min(piece, nodes - start))
+        fresh = own[rows] + step_size * late[rows]
+        new_register[rows] = fresh
+        pltpu.make_async_copy(new_register.at[rows], next_register.at[rows], sems.at[0]).start()
+        new_state[rows] = state[rows] + section_b * fresh
+        pltpu.make_async_copy(new_state.at[rows], next_state.at[rows], sems.at[1]).start()
+    pltpu.make_async_copy(new_register, next_register, sems.at[0]).wait()
+    pltpu.make_async_copy(new_state, next_state, sems.at[1]).wait()
+
+
 def body(curve_count, strip_count, state, register, neighbor, neighbor_face, seam):
     elems = neighbor.shape[1]
     columns = state.shape[2]
@@ -1032,6 +1098,7 @@
                 pltpu.VMEM((outer_levels * LANES, 4 * columns), bf16),
                 pltpu.VMEM((128, 4 * columns), f32),
                 pltpu.VMEM(shape, f32),
+                pltpu.SemaphoreType.REGULAR((reach,)),
                 pltpu.SemaphoreType.DMA,
                 pltpu.SemaphoreType.DMA((4,)),
                 pltpu.SemaphoreType.DMA,
@@ -1048,8 +1115,18 @@
         )
     else:
         own, late = two_rounds()
-    next_register = jnp.transpose(own, (1, 0, 2)) + step_size * jnp.transpose(late, (1, 0, 2))
-    return state + section_b * next_register, next_register
+    new = pl.pallas_call(
+        closing_kernel,
+        out_shape=(jax.ShapeDtypeStruct(shape, f32), jax.ShapeDtypeStruct(shape, f32)),
+        in_specs=[vmem] * 3,
+        out_specs=(pl.BlockSpec(memory_space=pl.ANY),) * 2,
+        scratch_shapes=[
+            pltpu.VMEM(shape, f32),
+            pltpu.VMEM(shape, f32),
+            pltpu.SemaphoreType.DMA((2,)),
+        ],
+    )(own, late, nodes_first)
+    return tuple(jnp.transpose(part, (1, 0, 2)) for part in new)
 
 
 def solution(mesh):

time: 11.8 us -> 11.5 us (0.975)
  other arithmetic: 0.75 us -> 0 us
  Pallas kernels: 10.2 us -> 10.6 us
    add x1 -> x0, other arithmetic: 0.75 us -> none  [body(): return (state + section_b * next_register, next_register)]
    pallas_call x0 -> x1, Pallas kernels: none -> 0.69 us  [body(): pl.pallas_call(closing_kernel, out_shape=(jax.ShapeDtypeStruct(shape, f32...]
    pallas_call x1, Pallas kernels: 10.2 us -> 9.94 us  [call(): pl.pallas_call(functools.partial(kernel, plan), out_shape=outputs, in_spe...]
where the time goes in v5:
time: 11.5 us; the launch traced here: 11.3 us
  Pallas kernels  10.6 us (92%)
  between operations  0.68 us (6%)
    pallas_call x1, Pallas kernels, call(): pl.pallas_call(functools.partial(kernel, plan), out_shape=outputs, in_spe...  9.94 us
    pallas_call x1, Pallas kernels, body(): pl.pallas_call(closing_kernel, out_shape=(jax.ShapeDtypeStruct(shape, f32...  0.69 us

profile of v5, /device:TPU:0, one launch (start us, length us, event | category | flops | bytes accessed | tf_op | source)
XLA Modules:
  0.0 11.3 jit_solution(1926973694173082957)
XLA Ops:
  0.6 0.0 copy-start
  0.6 0.0 copy-start.1
  0.6 9.9 %shard_map.97 = (f32[25,4,256]{2,1,0:T(4,128)S(1)}, f32[25,4,256]{2,1,0:T(4,128)S(1)}, s32[1]{0:T(128)S(4)}) custom-call(f32[25,4,256]{2,1,0:T(4,128)} %bitcast.5, s32[4,64]{1,0:T(4,128)} %neighbor_hbm.1, s32[4,64]{1,0:T(4,128)} %neighbor_face_hbm.1, s32[4,64]{1,0:T(4,128)} %seam_hbm.1, bf16[128,128]{1,0:T(8,128)(2,1)} %constant.11.clone.face_tables_hbm, ...), custom_call_target="tpu_custom_call" | custom-call | tf_op jit(solution)/shard_map/pallas_call | solution.py:1041
  10.6 0.0 copy-done
  10.6 0.0 copy-done.1
  10.6 0.7 %shard_map.98 = (f32[25,4,256]{2,1,0:T(4,128)}, f32[25,4,256]{2,1,0:T(4,128)}) custom-call(f32[25,4,256]{2,1,0:T(4,128)S(1)} %get-tuple-element.34.own, f32[25,4,256]{2,1,0:T(4,128)S(1)} %get-tuple-element.35.late, f32[25,4,256]{2,1,0:T(4,128)S(1)} %bitcast.7), custom_call_target="tpu_custom_call" | custom-call | tf_op jit(solution)/shard_map/pallas_call | solution.py:1118
  (1 shorter events, 0.0 us)
Async XLA Ops:
  0.6 10.0 %copy-start = (f32[4,25,256]{2,0,1:T(4,128)S(1)}, f32[4,25,256]{2,0,1:T(4,128)}, u32[]{:S(2)}) copy-start(f32[4,25,256]{2,0,1:T(4,128)} %param.10) | copy-start | bytes 307204
  0.6 10.0 %copy-start.1 = (f32[4,25,256]{2,0,1:T(4,128)S(1)}, f32[4,25,256]{2,0,1:T(4,128)}, u32[]{:S(2)}) copy-start(f32[4,25,256]{2,0,1:T(4,128)} %param.11) | copy-start | bytes 307204

commit v6 on v5

--- a/solution.py
+++ b/solution.py
@@ -500,7 +500,8 @@
     face_tables_hbm,
     tables_hbm,
     register_hbm,
-    own_part,
+    own_register,
+    own_state,
     late_part,
     sideways,
     state,
@@ -634,6 +635,7 @@
     for load in index_loads + state_loads + loads:
         load.start()
     notices[...] = jnp.zeros_like(notices)
+    verdict[...] = jnp.zeros_like(verdict)
     barrier = pltpu.get_barrier_semaphore()
     for index, place in enumerate(places):
         if beyond(index) is None:
@@ -663,9 +665,13 @@
     to_elem = iota((LANES, columns), 1) // levels
     reach = jnp.concatenate(
         [
-            onehot((from_elem < elems) & (from_elem < to_elem)),
-            onehot(from_elem < elems),
-            onehot(from_elem == to_elem),
+            jnp.concatenate(
+                [onehot((from_elem < elems) & (from_elem < to_elem)), onehot(from_elem < elems)],
+                axis=0,
+            ),
+            jnp.concatenate(
+                [onehot(from_elem == to_elem), onehot(from_elem < 0)], axis=0
+            ),
         ],
         axis=1,
     )
@@ -727,18 +733,19 @@
         jnp.concatenate([part, jnp.zeros_like(part)], axis=0)
         for part in (flipped.astype(f32), cosine, sine, side)
     ]
-    wide = dot(jnp.concatenate(member + extras, axis=0).astype(bf16), reach)
-    before = jnp.zeros((link_rows, columns), f32)
+    nothing = jnp.zeros_like(member[0])
+    before = [nothing, member[0], member[0] + member[1], member[0] + member[1] + member[2]]
+    left = jnp.concatenate(member + extras, axis=0).astype(bf16)
+    right = jnp.concatenate(before + [jnp.zeros_like(part) for part in extras], axis=0)
+    wide = dot(jnp.concatenate([left, right.astype(bf16)], axis=1), reach)
     spots = []
     for face in range(4):
         part = wide[face * link_rows : (face + 1) * link_rows]
-        rank = part[:, :columns] + before
-        before = before + part[:, columns : 2 * columns]
-        chosen = part[:, 2 * columns :] * (base_wide + inner * rank)
+        chosen = part[:, columns:] * (base_wide + inner * part[:, :columns])
         spots.append(jnp.sum(chosen, axis=0, keepdims=True))
     extra_row = 4 * link_rows
     flip_wide, cos_wide, sin_wide, side_wide = [
-        wide[extra_row + 8 * index : extra_row + 8 * index + 8, 2 * columns :]
+        wide[extra_row + 8 * index : extra_row + 8 * index + 8, columns:]
         for index in range(4)
     ]
 
@@ -747,7 +754,7 @@
         for values in per_face:
             rows.append(values)
             rows.append(jnp.zeros_like(values))
-        wide = dot(jnp.concatenate(rows, axis=0).astype(bf16), reach[:, 2 * columns :])
+        wide = dot(jnp.concatenate(rows, axis=0).astype(bf16), reach[:LANES, columns:])
         return [wide[8 * index : 8 * index + 8] for index in range(len(per_face))]
 
     def rows_for(slot, stride):
@@ -914,8 +921,11 @@
         held = jnp.concatenate([padded[field] for field in range(4)], axis=1)
         own = dot3(tables[:32, :288], jnp.concatenate([flux_x, flux_y, values], axis=0))
         own = section_a * held + step_size * own
+        moved = values + section_b * own
         for field in range(4):
-            own_part[:, field, :] = own[:25, field * columns : (field + 1) * columns]
+            sides = slice(field * columns, (field + 1) * columns)
+            own_register[:, field, :] = own[:25, sides]
+            own_state[:, field, :] = moved[:25, sides]
 
     for index in order:
         if before_start(index) is not None:
@@ -962,53 +972,67 @@
             rows.append(term if drops[field] is None else term + drops[field])
         terms.append(jnp.concatenate(rows, axis=0))
     face_term = jnp.concatenate(terms, axis=1)
+
+    @pl.when(collects)
+    def _():
+        rows_done(notices, device_count - 1, notice_recv_sem).wait()
+
+        @pl.when(device_pos == herald)
+        def _():
+            heard = jnp.max(notices[...], axis=0, keepdims=True) + notice[:1]
+            notice[8:] = jnp.broadcast_to(heard, (8, LANES))
+            for position in range(device_count):
+                if position not in collectors:
+                    verdict_to(position).start()
+
+    @pl.when(jnp.logical_not(collects))
+    def _():
+        rows_done(verdict, 1, verdict_recv_sem).wait()
+
+    heard = jnp.maximum(notice[:8], verdict[...])
+    for start in range(0, notices.shape[0], 8):
+        heard = jnp.maximum(heard, notices[start : start + 8])
+    sideways[0] = jnp.where(jnp.max(heard) > 0.5, 1, 0)
     late = dot3(
         tables[32:, :192], jnp.concatenate([to_faces(face_term), to_faces(jump)], axis=0)
     )
     for field in range(4):
         late_part[:, field, :] = late[:25, field * columns : (field + 1) * columns]
 
+    @pl.when(device_pos == herald)
+    def _():
+        rows_done(notices, device_count - len(collectors), verdict_send_sem).wait()
+
     @pl.when(collects)
     def _():
-        rows_done(notices, device_count - 1, notice_recv_sem).wait()
-        heard = jnp.max(notices[...], axis=0, keepdims=True) + notice[:1]
-        notice[8:] = jnp.broadcast_to(heard, (8, LANES))
-
-        @pl.when(device_pos == herald)
-        def _():
-            for position in range(device_count):
-                if position not in collectors:
-                    verdict_to(position).start()
-
-        sideways[0] = jnp.where(jnp.max(heard) > 0.5, 1, 0)
-
-        @pl.when(device_pos == herald)
-        def _():
-            rows_done(notices, device_count - len(collectors), verdict_send_sem).wait()
-
         rows_done(notice, len(collectors) - 1, notice_send_sem).wait()
 
     @pl.when(jnp.logical_not(collects))
     def _():
         rows_done(notice, len(collectors), notice_send_sem).wait()
-        rows_done(verdict, 1, verdict_recv_sem).wait()
-        sideways[0] = jnp.where(jnp.max(verdict[:1]) > 0.5, 1, 0)
 
     rows_done(sent, total_rows, send_sem).wait()
 
 
-def closing_kernel(own, late, state, next_state, next_register, new_state, new_register, sems):
-    nodes = own.shape[0]
+def closing_kernel(
+    own_register, own_state, late, next_state, next_register, new_state, new_register, sems
+):
+    nodes = late.shape[0]
     piece = -(-nodes // 3)
     for start in range(0, nodes, piece):
         rows = pl.ds(start, min(piece, nodes - start))
-        fresh = own[rows] + step_size * late[rows]
-        new_register[rows] = fresh
+        part = step_size * late[rows]
+        new_register[rows] = own_register[rows] + part
         pltpu.make_async_copy(new_register.at[rows], next_register.at[rows], sems.at[0]).start()
-        new_state[rows] = state[rows] + section_b * fresh
+        new_state[rows] = own_state[rows] + section_b * part
         pltpu.make_async_copy(new_state.at[rows], next_state.at[rows], sems.at[1]).start()
     pltpu.make_async_copy(new_register, next_register, sems.at[0]).wait()
     pltpu.make_async_copy(new_state, next_state, sems.at[1]).wait()
+
+
+def start_kernel(state, register, own_register, own_state):
+    own_register[...] = section_a * register[...]
+    own_state[...] = state[...] + section_b * own_register[...]
 
 
 def body(curve_count, strip_count, state, register, neighbor, neighbor_face, seam):
@@ -1074,7 +1098,13 @@
             ],
             0,
         )
-        return section_a * register_first, change
+        started = pl.pallas_call(
+            start_kernel,
+            out_shape=(pltpu.VMEM(shape, f32), pltpu.VMEM(shape, f32)),
+            in_specs=[vmem, vmem],
+            out_specs=(vmem, vmem),
+        )(*[pltpu.with_memory_space_constraint(x, pltpu.HBM) for x in (nodes_first, register_first)])
+        return *started, change
 
     device_count = curve_count * strip_count
     if device_count <= DIRECT_LIMIT and total_rows <= LANES and outer_levels * 64 == LANES:
@@ -1082,8 +1112,8 @@
             direct_kernel,
             build_direct_tables(),
             (register_first,),
-            (pltpu.VMEM(shape, f32), pltpu.VMEM(shape, f32), pltpu.SMEM((1,), jnp.int32)),
-            (vmem, vmem, pl.BlockSpec(memory_space=pltpu.SMEM)),
+            (pltpu.VMEM(shape, f32),) * 3 + (pltpu.SMEM((1,), jnp.int32),),
+            (vmem,) * 3 + (pl.BlockSpec(memory_space=pltpu.SMEM),),
             [
                 pltpu.VMEM(shape, f32),
                 pltpu.VMEM((3, *neighbor.shape), jnp.int32),
@@ -1110,11 +1140,11 @@
             ],
             1,
         )
-        own, late = lax.cond(
+        parts = lax.cond(
             sideways[0] == 0, lambda kept: tuple(kept), lambda _: two_rounds(), parts
         )
     else:
-        own, late = two_rounds()
+        parts = two_rounds()
     new = pl.pallas_call(
         closing_kernel,
         out_shape=(jax.ShapeDtypeStruct(shape, f32), jax.ShapeDtypeStruct(shape, f32)),
@@ -1125,7 +1155,7 @@
             pltpu.VMEM(shape, f32),
             pltpu.SemaphoreType.DMA((2,)),
         ],
-    )(own, late, nodes_first)
+    )(*parts)
     return tuple(jnp.transpose(part, (1, 0, 2)) for part in new)
 
 

time: 11.5 us -> 11.3 us (0.983)
    pallas_call x1, Pallas kernels: 9.94 us -> 9.79 us  [call(): pl.pallas_call(functools.partial(kernel, plan), out_shape=outputs, in_spe...]
where the time goes in v6:
time: 11.3 us; the launch traced here: 11.1 us
  Pallas kernels  10.5 us (93%)
  between operations  0.65 us (6%)
    pallas_call x1, Pallas kernels, call(): pl.pallas_call(functools.partial(kernel, plan), out_shape=outputs, in_spe...  9.79 us
    pallas_call x1, Pallas kernels, body(): pl.pallas_call(closing_kernel, out_shape=(jax.ShapeDtypeStruct(shape, f32...  0.69 us

profile of v6, /device:TPU:0, one launch (start us, length us, event | category | flops | bytes accessed | tf_op | source)
XLA Modules:
  0.0 11.1 jit_solution(13522056041547224245)
XLA Ops:
  0.6 9.8 %shard_map.97 = (f32[25,4,256]{2,1,0:T(4,128)S(1)}, f32[25,4,256]{2,1,0:T(4,128)S(1)}, f32[25,4,256]{2,1,0:T(4,128)S(1)}, s32[1]{0:T(128)S(4)}) custom-call(f32[25,4,256]{2,1,0:T(4,128)} %bitcast.5, s32[4,64]{1,0:T(4,128)} %neighbor_hbm.1, s32[4,64]{1,0:T(4,128)} %neighbor_face_hbm.1, s32[4,64]{1,0:T(4,128)} %seam_hbm.1, ...), custom_call_target="tpu_custom_call" | custom-call | tf_op jit(solution)/shard_map/pallas_call | solution.py:1065
  10.4 0.7 %shard_map.98 = (f32[25,4,256]{2,1,0:T(4,128)}, f32[25,4,256]{2,1,0:T(4,128)}) custom-call(f32[25,4,256]{2,1,0:T(4,128)S(1)} %get-tuple-element.41.own_register, f32[25,4,256]{2,1,0:T(4,128)S(1)} %get-tuple-element.42.own_state, f32[25,4,256]{2,1,0:T(4,128)S(1)} %get-tuple-element.43.late), custom_call_target="tpu_custom_call" | custom-call | tf_op jit(solution)/shard_map/pallas_call | solution.py:1148
  (1 shorter events, 0.0 us)

commit v7 on v6

--- a/solution.py
+++ b/solution.py
@@ -609,7 +609,7 @@
         )
 
     index_loads = [
-        pltpu.make_async_copy(source_ref, indices.at[index], index_sem)
+        pltpu.make_async_copy(source_ref, indices.at[index], index_sem.at[index // 2])
         for index, source_ref in enumerate((neighbor_face_hbm, seam_hbm, neighbor_hbm))
     ]
     loads = [
@@ -635,7 +635,6 @@
     for load in index_loads + state_loads + loads:
         load.start()
     notices[...] = jnp.zeros_like(notices)
-    verdict[...] = jnp.zeros_like(verdict)
     barrier = pltpu.get_barrier_semaphore()
     for index, place in enumerate(places):
         if beyond(index) is None:
@@ -675,13 +674,12 @@
         ],
         axis=1,
     )
-    pltpu.make_async_copy(indices, indices, index_sem).wait()
-
-    face_back, codes, across = [
-        jnp.concatenate([indices[index]] * inner, axis=1) for index in range(3)
+    pair = indices.at[pl.ds(0, 2)]
+    pltpu.make_async_copy(pair, pair, index_sem.at[0]).wait()
+
+    face_back, codes = [
+        jnp.concatenate([indices[index]] * inner, axis=1) for index in range(2)
     ]
-    owner = across // elems
-    place_in = across % elems
     turn = codes % 4
     flipped = codes // 4
     own_face = iota((4, LANES), 0)
@@ -724,8 +722,12 @@
     cosine = jnp.where(turn == 0, 1.0, 0.0) - jnp.where(turn == 2, 1.0, 0.0)
     sine = jnp.where(turn == 3, 1.0, 0.0) - jnp.where(turn == 1, 1.0, 0.0)
 
+    index_loads[2].wait()
     loads[0].wait()
     pltpu.make_async_copy(state, state, load_sem.at[3]).wait()
+    across = jnp.concatenate([indices[2]] * inner, axis=1)
+    owner = across // elems
+    place_in = across % elems
     member = [
         jnp.where(owner[face : face + 1] == target, 1.0, 0.0) for face in range(4)
     ]
@@ -985,11 +987,7 @@
                 if position not in collectors:
                     verdict_to(position).start()
 
-    @pl.when(jnp.logical_not(collects))
-    def _():
-        rows_done(verdict, 1, verdict_recv_sem).wait()
-
-    heard = jnp.maximum(notice[:8], verdict[...])
+    heard = notice[:8]
     for start in range(0, notices.shape[0], 8):
         heard = jnp.maximum(heard, notices[start : start + 8])
     sideways[0] = jnp.where(jnp.max(heard) > 0.5, 1, 0)
@@ -1010,6 +1008,8 @@
     @pl.when(jnp.logical_not(collects))
     def _():
         rows_done(notice, len(collectors), notice_send_sem).wait()
+        rows_done(verdict, 1, verdict_recv_sem).wait()
+        sideways[0] = jnp.where(jnp.max(verdict[:1]) > 0.5, 1, 0)
 
     rows_done(sent, total_rows, send_sem).wait()
 
@@ -1129,7 +1129,7 @@
                 pltpu.VMEM((128, 4 * columns), f32),
                 pltpu.VMEM(shape, f32),
                 pltpu.SemaphoreType.REGULAR((reach,)),
-                pltpu.SemaphoreType.DMA,
+                pltpu.SemaphoreType.DMA((2,)),
                 pltpu.SemaphoreType.DMA((4,)),
                 pltpu.SemaphoreType.DMA,
                 pltpu.SemaphoreType.DMA,

time: 11.3 us -> 11.3 us (level)
  no operation moved by 1% of the time
where the time goes in v7:
time: 11.3 us; the launch traced here: 11.1 us
  Pallas kernels  10.5 us (93%)
  between operations  0.65 us (6%)
    pallas_call x1, Pallas kernels, call(): pl.pallas_call(functools.partial(kernel, plan), out_shape=outputs, in_spe...  9.76 us
    pallas_call x1, Pallas kernels, body(): pl.pallas_call(closing_kernel, out_shape=(jax.ShapeDtypeStruct(shape, f32...  0.69 us

profile of v7, /device:TPU:0, one launch (start us, length us, event | category | flops | bytes accessed | tf_op | source)
XLA Modules:
  0.0 11.1 jit_solution(6398119142956510194)
XLA Ops:
  0.6 9.8 %shard_map.97 = (f32[25,4,256]{2,1,0:T(4,128)S(1)}, f32[25,4,256]{2,1,0:T(4,128)S(1)}, f32[25,4,256]{2,1,0:T(4,128)S(1)}, s32[1]{0:T(128)S(4)}) custom-call(f32[25,4,256]{2,1,0:T(4,128)} %bitcast.5, s32[4,64]{1,0:T(4,128)} %neighbor_hbm.1, s32[4,64]{1,0:T(4,128)} %neighbor_face_hbm.1, s32[4,64]{1,0:T(4,128)} %seam_hbm.1, ...), custom_call_target="tpu_custom_call" | custom-call | tf_op jit(solution)/shard_map/pallas_call | solution.py:1065
  10.4 0.7 %shard_map.98 = (f32[25,4,256]{2,1,0:T(4,128)}, f32[25,4,256]{2,1,0:T(4,128)}) custom-call(f32[25,4,256]{2,1,0:T(4,128)S(1)} %get-tuple-element.41.own_register, f32[25,4,256]{2,1,0:T(4,128)S(1)} %get-tuple-element.42.own_state, f32[25,4,256]{2,1,0:T(4,128)S(1)} %get-tuple-element.43.late), custom_call_target="tpu_custom_call" | custom-call | tf_op jit(solution)/shard_map/pallas_call | solution.py:1148
  (1 shorter events, 0.0 us)

commit v8 on v7

--- a/solution.py
+++ b/solution.py
@@ -523,9 +523,8 @@
     send_sem,
     recv_sem,
     notice_send_sem,
-    notice_recv_sem,
+    word_recv_sem,
     verdict_send_sem,
-    verdict_recv_sem,
 ):
     elems, levels, curve_count, strip_count, links, rows_of, offsets = plan
     columns = elems * levels
@@ -578,7 +577,7 @@
             src_ref=notice.at[pl.ds(0, 1)],
             dst_ref=notices.at[pl.ds(device_pos, 1)],
             send_sem=notice_send_sem,
-            recv_sem=notice_recv_sem,
+            recv_sem=word_recv_sem,
             device_id=place_of(position),
             device_id_type=pl.DeviceIdType.MESH,
         )
@@ -588,7 +587,7 @@
             src_ref=notice.at[pl.ds(8, 1)],
             dst_ref=verdict.at[pl.ds(0, 1)],
             send_sem=verdict_send_sem,
-            recv_sem=verdict_recv_sem,
+            recv_sem=word_recv_sem,
             device_id=place_of(position),
             device_id_type=pl.DeviceIdType.MESH,
         )
@@ -700,7 +699,7 @@
                 @pl.when(beyond(index))
                 def _():
                     pl.semaphore_signal(
-                        ready.at[links[index][1] - 1],
+                        ready,
                         inc=1,
                         device_id=places[index],
                         device_id_type=pl.DeviceIdType.MESH,
@@ -929,13 +928,15 @@
             own_register[:, field, :] = own[:25, sides]
             own_state[:, field, :] = moved[:25, sides]
 
-    for index in order:
-        if before_start(index) is not None:
-
-            @pl.when(before_start(index))
-            def _():
-                pl.semaphore_wait(ready.at[-links[index][1] - 1], 1)
-                copy_of(index).start()
+    waiting = [index for index in order if before_start(index) is not None]
+    late_partners = sum(jnp.where(before_start(index), 1, 0) for index in waiting)
+
+    @pl.when(late_partners > 0)
+    def _():
+        pl.semaphore_wait(ready, late_partners)
+
+    for index in waiting:
+        pl.when(before_start(index))(copy_of(index).start)
 
     rows_done(arrived, total_rows, recv_sem).wait()
     filler = jnp.zeros((LANES - total_rows, LANES), f32)
@@ -977,7 +978,7 @@
 
     @pl.when(collects)
     def _():
-        rows_done(notices, device_count - 1, notice_recv_sem).wait()
+        rows_done(notices, device_count - 1, word_recv_sem).wait()
 
         @pl.when(device_pos == herald)
         def _():
@@ -1008,7 +1009,7 @@
     @pl.when(jnp.logical_not(collects))
     def _():
         rows_done(notice, len(collectors), notice_send_sem).wait()
-        rows_done(verdict, 1, verdict_recv_sem).wait()
+        rows_done(verdict, 1, word_recv_sem).wait()
         sideways[0] = jnp.where(jnp.max(verdict[:1]) > 0.5, 1, 0)
 
     rows_done(sent, total_rows, send_sem).wait()
@@ -1128,10 +1129,9 @@
                 pltpu.VMEM((outer_levels * LANES, 4 * columns), bf16),
                 pltpu.VMEM((128, 4 * columns), f32),
                 pltpu.VMEM(shape, f32),
-                pltpu.SemaphoreType.REGULAR((reach,)),
+                pltpu.SemaphoreType.REGULAR,
                 pltpu.SemaphoreType.DMA((2,)),
                 pltpu.SemaphoreType.DMA((4,)),
-                pltpu.SemaphoreType.DMA,
                 pltpu.SemaphoreType.DMA,
                 pltpu.SemaphoreType.DMA,
                 pltpu.SemaphoreType.DMA,

time: 11.3 us -> 11.2 us (level)
  no operation moved by 1% of the time
where the time goes in v8:
time: 11.2 us; the launch traced here: 11.1 us
  Pallas kernels  10.4 us (93%)
  between operations  0.65 us (6%)
    pallas_call x1, Pallas kernels, call(): pl.pallas_call(functools.partial(kernel, plan), out_shape=outputs, in_spe...  9.74 us
    pallas_call x1, Pallas kernels, body(): pl.pallas_call(closing_kernel, out_shape=(jax.ShapeDtypeStruct(shape, f32...  0.69 us

profile of v8, /device:TPU:0, one launch (start us, length us, event | category | flops | bytes accessed | tf_op | source)
XLA Modules:
  0.0 11.1 jit_solution(104915077801076103)
XLA Ops:
  0.6 9.7 %shard_map.97 = (f32[25,4,256]{2,1,0:T(4,128)S(1)}, f32[25,4,256]{2,1,0:T(4,128)S(1)}, f32[25,4,256]{2,1,0:T(4,128)S(1)}, s32[1]{0:T(128)S(4)}) custom-call(f32[25,4,256]{2,1,0:T(4,128)} %bitcast.5, s32[4,64]{1,0:T(4,128)} %neighbor_hbm.1, s32[4,64]{1,0:T(4,128)} %neighbor_face_hbm.1, s32[4,64]{1,0:T(4,128)} %seam_hbm.1, ...), custom_call_target="tpu_custom_call" | custom-call | tf_op jit(solution)/shard_map/pallas_call | solution.py:1066
  10.4 0.7 %shard_map.98 = (f32[25,4,256]{2,1,0:T(4,128)}, f32[25,4,256]{2,1,0:T(4,128)}) custom-call(f32[25,4,256]{2,1,0:T(4,128)S(1)} %get-tuple-element.41.own_register, f32[25,4,256]{2,1,0:T(4,128)S(1)} %get-tuple-element.42.own_state, f32[25,4,256]{2,1,0:T(4,128)S(1)} %get-tuple-element.43.late), custom_call_target="tpu_custom_call" | custom-call | tf_op jit(solution)/shard_map/pallas_call | solution.py:1148
  (1 shorter events, 0.0 us)

commit v9 on v8

--- a/solution.py
+++ b/solution.py
@@ -555,6 +555,12 @@
     def place_of(position):
         return (position // strip_count, position % strip_count)
 
+    tile_rows = 4 * columns // LANES
+
+    def sides_of(row):
+        start = row % 4 * columns + row // 4 * LANES
+        return slice(start, start + LANES)
+
     def beyond(index):
         axis, step = links[index]
         if axis == "curve" and step > 0:
@@ -608,7 +614,7 @@
         )
 
     index_loads = [
-        pltpu.make_async_copy(source_ref, indices.at[index], index_sem.at[index // 2])
+        pltpu.make_async_copy(source_ref, indices.at[index], index_sem)
         for index, source_ref in enumerate((neighbor_face_hbm, seam_hbm, neighbor_hbm))
     ]
     loads = [
@@ -673,8 +679,7 @@
         ],
         axis=1,
     )
-    pair = indices.at[pl.ds(0, 2)]
-    pltpu.make_async_copy(pair, pair, index_sem.at[0]).wait()
+    pltpu.make_async_copy(indices, indices, index_sem).wait()
 
     face_back, codes = [
         jnp.concatenate([indices[index]] * inner, axis=1) for index in range(2)
@@ -721,7 +726,6 @@
     cosine = jnp.where(turn == 0, 1.0, 0.0) - jnp.where(turn == 2, 1.0, 0.0)
     sine = jnp.where(turn == 3, 1.0, 0.0) - jnp.where(turn == 1, 1.0, 0.0)
 
-    index_loads[2].wait()
     loads[0].wait()
     pltpu.make_async_copy(state, state, load_sem.at[3]).wait()
     across = jnp.concatenate([indices[2]] * inner, axis=1)
@@ -923,10 +927,9 @@
         own = dot3(tables[:32, :288], jnp.concatenate([flux_x, flux_y, values], axis=0))
         own = section_a * held + step_size * own
         moved = values + section_b * own
-        for field in range(4):
-            sides = slice(field * columns, (field + 1) * columns)
-            own_register[:, field, :] = own[:25, sides]
-            own_state[:, field, :] = moved[:25, sides]
+        for row in range(tile_rows):
+            own_register[:, row, :] = own[:25, sides_of(row)]
+            own_state[:, row, :] = moved[:25, sides_of(row)]
 
     waiting = [index for index in order if before_start(index) is not None]
     late_partners = sum(jnp.where(before_start(index), 1, 0) for index in waiting)
@@ -995,8 +998,8 @@
     late = dot3(
         tables[32:, :192], jnp.concatenate([to_faces(face_term), to_faces(jump)], axis=0)
     )
-    for field in range(4):
-        late_part[:, field, :] = late[:25, field * columns : (field + 1) * columns]
+    for row in range(tile_rows):
+        late_part[:, row, :] = late[:25, sides_of(row)]
 
     @pl.when(device_pos == herald)
     def _():
@@ -1059,6 +1062,16 @@
     nodes_first = jnp.transpose(state, (1, 0, 2))
     register_first = jnp.transpose(register, (1, 0, 2))
     shape = nodes_first.shape
+    tiled = (shape[0], 4 * columns // LANES, LANES)
+
+    def to_tiles(x):
+        split = x.reshape(shape[0], 4, columns // LANES, LANES)
+        return jnp.transpose(split, (0, 2, 1, 3)).reshape(tiled)
+
+    def from_tiles(x):
+        split = x.reshape(shape[0], columns // LANES, 4, LANES)
+        return jnp.transpose(split, (2, 0, 1, 3)).reshape(4, shape[0], columns)
+
 
     def call(kernel, tables, more, outputs, out_specs, scratch, collective_id):
         tables = [jnp.asarray(table) for table in tables]
@@ -1101,11 +1114,11 @@
         )
         started = pl.pallas_call(
             start_kernel,
-            out_shape=(pltpu.VMEM(shape, f32), pltpu.VMEM(shape, f32)),
+            out_shape=(pltpu.VMEM(tiled, f32), pltpu.VMEM(tiled, f32)),
             in_specs=[vmem, vmem],
             out_specs=(vmem, vmem),
-        )(*[pltpu.with_memory_space_constraint(x, pltpu.HBM) for x in (nodes_first, register_first)])
-        return *started, change
+        )(*[pltpu.with_memory_space_constraint(x, pltpu.HBM) for x in (to_tiles(nodes_first), to_tiles(register_first))])
+        return *started, to_tiles(change)
 
     device_count = curve_count * strip_count
     if device_count <= DIRECT_LIMIT and total_rows <= LANES and outer_levels * 64 == LANES:
@@ -1113,7 +1126,7 @@
             direct_kernel,
             build_direct_tables(),
             (register_first,),
-            (pltpu.VMEM(shape, f32),) * 3 + (pltpu.SMEM((1,), jnp.int32),),
+            (pltpu.VMEM(tiled, f32),) * 3 + (pltpu.SMEM((1,), jnp.int32),),
             (vmem,) * 3 + (pl.BlockSpec(memory_space=pltpu.SMEM),),
             [
                 pltpu.VMEM(shape, f32),
@@ -1130,7 +1143,7 @@
                 pltpu.VMEM((128, 4 * columns), f32),
                 pltpu.VMEM(shape, f32),
                 pltpu.SemaphoreType.REGULAR,
-                pltpu.SemaphoreType.DMA((2,)),
+                pltpu.SemaphoreType.DMA,
                 pltpu.SemaphoreType.DMA((4,)),
                 pltpu.SemaphoreType.DMA,
                 pltpu.SemaphoreType.DMA,
@@ -1147,16 +1160,16 @@
         parts = two_rounds()
     new = pl.pallas_call(
         closing_kernel,
-        out_shape=(jax.ShapeDtypeStruct(shape, f32), jax.ShapeDtypeStruct(shape, f32)),
+        out_shape=(jax.ShapeDtypeStruct(tiled, f32), jax.ShapeDtypeStruct(tiled, f32)),
         in_specs=[vmem] * 3,
         out_specs=(pl.BlockSpec(memory_space=pl.ANY),) * 2,
         scratch_shapes=[
-            pltpu.VMEM(shape, f32),
-            pltpu.VMEM(shape, f32),
+            pltpu.VMEM(tiled, f32),
+            pltpu.VMEM(tiled, f32),
             pltpu.SemaphoreType.DMA((2,)),
         ],
     )(*parts)
-    return tuple(jnp.transpose(part, (1, 0, 2)) for part in new)
+    return tuple(from_tiles(part) for part in new)
 
 
 def solution(mesh):

time: 11.2 us -> 11.3 us (level)
  no operation moved by 1% of the time
where the time goes in v9:
time: 11.3 us; the launch traced here: 11.1 us
  Pallas kernels  10.5 us (93%)
  between operations  0.65 us (6%)
    pallas_call x1, Pallas kernels, call(): pl.pallas_call(functools.partial(kernel, plan), out_shape=outputs, in_spe...  9.79 us
    pallas_call x1, Pallas kernels, body(): pl.pallas_call(closing_kernel, out_shape=(jax.ShapeDtypeStruct(tiled, f32...  0.69 us

profile of v9, /device:TPU:0, one launch (start us, length us, event | category | flops | bytes accessed | tf_op | source)
XLA Modules:
  0.0 11.1 jit_solution(3166327127221047111)
XLA Ops:
  0.6 9.8 %shard_map.97 = (f32[25,8,128]{2,1,0:T(8,128)S(1)}, f32[25,8,128]{2,1,0:T(8,128)S(1)}, f32[25,8,128]{2,1,0:T(8,128)S(1)}, s32[1]{0:T(128)S(4)}) custom-call(f32[25,4,256]{2,1,0:T(4,128)} %bitcast.26, s32[4,64]{1,0:T(4,128)} %neighbor_hbm.1, s32[4,64]{1,0:T(4,128)} %neighbor_face_hbm.1, s32[4,64]{1,0:T(4,128)} %seam_hbm.1, ...), custom_call_target="tpu_custom_call" | custom-call | tf_op jit(solution)/shard_map/pallas_call | solution.py:1079
  10.5 0.7 %shard_map.98 = (f32[25,8,128]{2,1,0:T(8,128)}, f32[25,8,128]{2,1,0:T(8,128)}) custom-call(f32[25,8,128]{2,1,0:T(8,128)S(1)} %get-tuple-element.41.own_register, f32[25,8,128]{2,1,0:T(8,128)S(1)} %get-tuple-element.42.own_state, f32[25,8,128]{2,1,0:T(8,128)S(1)} %get-tuple-element.43.late), custom_call_target="tpu_custom_call" | custom-call | tf_op jit(solution)/shard_map/pallas_call | solution.py:1161
  (1 shorter events, 0.0 us)
